TPU v7x, 32 devices: a whole 2x2x4 slice. The times are simulated.
32 devices in a mesh: dp: 2 (over x), col: 4 (over z), row: 4 (over y, core).
Axes of the slice: x: 2, y: 2, z: 4, core: 2. Of those that a mesh axis runs over, the one named last changes fastest.
Arguments:
- x_in: bfloat16 [8, 768, 2048], P(('dp', 'row'), None, 'col'), parts along dimension 0
- ln1_scale: float32 [2048], P('col')
- ln1_shift: float32 [2048], P('col')
- w_qkv: bfloat16 [2048, 6144], P('row', 'col')
- b_qkv: float32 [32, 192], P('col')
- w_o: bfloat16 [2048, 2048], P('row', 'col')
- b_o: float32 [2048], P('col')
- ln2_scale: float32 [2048], P('col')
- ln2_shift: float32 [2048], P('col')
- w_in: bfloat16 [2048, 8192], P('row', 'col')
- b_in: float32 [8192], P('col')
- w_out: bfloat16 [8192, 2048], P('row', 'col')
- b_out: float32 [2048], P('col')
- grad_out: bfloat16 [8, 768, 2048], P(('dp', 'row'), None, 'col'), parts along dimension 0
Outputs:
- output 1: bfloat16 [8, 768, 2048], P(('dp', 'row'), None, 'col'), parts along dimension 0
- output 2: bfloat16 [8, 768, 2048], P(('dp', 'row'), None, 'col'), parts along dimension 0
- output 3: float32 [4096], P(('dp', 'col')), parts along dimension 0
- output 4: float32 [4096], P(('dp', 'col')), parts along dimension 0
- output 5: bfloat16 [4096, 6144], P(('dp', 'row'), 'col'), parts along dimension 0
- output 6: float32 [64, 192], P(('dp', 'col')), parts along dimension 0
- output 7: bfloat16 [4096, 2048], P(('dp', 'row'), 'col'), parts along dimension 0
- output 8: float32 [4096], P(('dp', 'col')), parts along dimension 0
- output 9: float32 [4096], P(('dp', 'col')), parts along dimension 0
- output 10: float32 [4096], P(('dp', 'col')), parts along dimension 0
- output 11: bfloat16 [4096, 8192], P(('dp', 'row'), 'col'), parts along dimension 0
- output 12: float32 [16384], P(('dp', 'col')), parts along dimension 0
- output 13: bfloat16 [16384, 2048], P(('dp', 'row'), 'col'), parts along dimension 0
- output 14: float32 [4096], P(('dp', 'col')), parts along dimension 0
There are 2 independent parts. A program takes and returns all parts, laid end to end along the dimension named above; an argument that names none is the same for every part.
All inputs are finite; a program needn't handle non-finite values.
Results may differ from a plain program's by a relative error of at most 0.0113486.
Values are sent between devices in bfloat16 or wider.
A program may use at most 1 GiB of HBM per device.

v0:
```python
import jax
import jax.numpy as jnp
from jax import lax
from jax.sharding import PartitionSpec as P

LN_EPS = 1e-5


def gelu_tanh(pre_act):
    return jax.nn.gelu(pre_act, approximate=True)


def attend_one(query_rows, key_rows, value_rows):
    seq_len, head_dim = query_rows.shape
    scores = lax.dot_general(query_rows, key_rows, (((1,), (1,)), ((), ())), preferred_element_type=jnp.float32)
    query_pos = lax.broadcasted_iota(jnp.int32, (seq_len, 1), 0)
    key_pos = lax.broadcasted_iota(jnp.int32, (1, seq_len), 1)
    attn_probs = jax.nn.softmax(jnp.where(key_pos <= query_pos, scores * head_dim ** -0.5, -1e30), axis=-1)
    return jnp.dot(attn_probs.astype(jnp.bfloat16), value_rows, preferred_element_type=jnp.float32).astype(jnp.bfloat16)


def attend_item(head_item):
    return attend_one(head_item[0], head_item[1], head_item[2])


def attend_item_back(item_pair):
    head_item, grad_item = item_pair
    pullback = jax.vjp(attend_one, head_item[0], head_item[1], head_item[2])[1]
    return jnp.stack(pullback(grad_item))


def layer_norm_fwd(act_blk, ln_scale, ln_shift, feat_width):
    act_f32 = act_blk.astype(jnp.float32)
    ln_stats = jnp.stack([jnp.sum(act_f32, axis=-1), jnp.sum(act_f32 * act_f32, axis=-1)], axis=-1)
    ln_stats = lax.psum(ln_stats, 'col') / feat_width
    mean_val = ln_stats[:, 0:1]
    inv_std = lax.rsqrt(ln_stats[:, 1:2] - mean_val * mean_val + LN_EPS)
    normed = (act_f32 - mean_val) * inv_std
    return (normed * ln_scale + ln_shift).astype(jnp.bfloat16), normed, inv_std


def layer_norm_bwd(grad_blk, normed, inv_std, ln_scale, feat_width):
    grad_f32 = grad_blk.astype(jnp.float32)
    grad_scale = lax.psum(jnp.sum(grad_f32 * normed, axis=0), 'row')
    grad_shift = lax.psum(jnp.sum(grad_f32, axis=0), 'row')
    grad_hat = grad_f32 * ln_scale
    grad_sums = jnp.stack([jnp.sum(grad_hat, axis=-1), jnp.sum(grad_hat * normed, axis=-1)], axis=-1)
    grad_sums = lax.psum(grad_sums, 'col') / feat_width
    grad_in = inv_std * (grad_hat - grad_sums[:, 0:1] - normed * grad_sums[:, 1:2])
    return grad_in, grad_scale, grad_shift


def gather_weight(w_blk):
    return lax.all_gather(w_blk, 'row', axis=0, tiled=True)


def gather_features(act_blk):
    return lax.all_gather(act_blk, 'col', axis=1, tiled=True)


def matmul_fwd(act_blk, w_blk):
    return jnp.dot(gather_features(act_blk), gather_weight(w_blk), preferred_element_type=jnp.float32)


def matmul_bwd(act_blk, w_blk, grad_blk):
    part_act = lax.dot_general(grad_blk, gather_weight(w_blk), (((1,), (1,)), ((), ())), preferred_element_type=jnp.float32)
    grad_act = lax.psum_scatter(part_act, 'col', scatter_dimension=1, tiled=True)
    part_w = lax.dot_general(gather_features(act_blk), grad_blk, (((0,), (0,)), ((), ())), preferred_element_type=jnp.float32)
    grad_w = lax.psum_scatter(part_w, 'row', scatter_dimension=0, tiled=True)
    return grad_act, grad_w.astype(jnp.bfloat16)


def bias_grad(grad_blk):
    return lax.psum(jnp.sum(grad_blk.astype(jnp.float32), axis=0), 'row')


def solution(mesh):
    col_size = mesh.shape['col']
    act_spec = P(('dp', 'row'), None, 'col')
    vec_spec = P('col')
    mat_spec = P('row', 'col')
    head_spec = P('col', None)
    gvec_spec = P(('dp', 'col'))
    gmat_spec = P(('dp', 'row'), 'col')
    ghead_spec = P(('dp', 'col'), None)

    def layer_block(x_blk, ln1_scale, ln1_shift, w_qkv, b_qkv, w_o, b_o, ln2_scale, ln2_shift, w_in, b_in, w_out, b_out, grad_blk):
        seq_count, seq_len, d_local = x_blk.shape
        tokens = seq_count * seq_len
        heads_local, qkv_width = b_qkv.shape
        head_dim = qkv_width // 3
        feat_width = d_local * col_size
        x_rows = x_blk.reshape(tokens, d_local)
        normed1, ln1_hat, ln1_inv = layer_norm_fwd(x_rows, ln1_scale, ln1_shift, feat_width)
        qkv_rows = (matmul_fwd(normed1, w_qkv) + b_qkv.reshape(heads_local * qkv_width)).astype(jnp.bfloat16)
        head_items = qkv_rows.reshape(seq_count, seq_len, heads_local, 3, head_dim).transpose(0, 2, 3, 1, 4).reshape(seq_count * heads_local, 3, seq_len, head_dim)
        attn_items = lax.map(attend_item, head_items)
        attn_rows = attn_items.reshape(seq_count, heads_local, seq_len, head_dim).transpose(0, 2, 1, 3).reshape(tokens, d_local)
        resid_rows = (x_rows.astype(jnp.float32) + matmul_fwd(attn_rows, w_o) + b_o).astype(jnp.bfloat16)
        normed2, ln2_hat, ln2_inv = layer_norm_fwd(resid_rows, ln2_scale, ln2_shift, feat_width)
        pre_act = matmul_fwd(normed2, w_in) + b_in
        hidden = gelu_tanh(pre_act).astype(jnp.bfloat16)
        out_rows = (resid_rows.astype(jnp.float32) + matmul_fwd(hidden, w_out) + b_out).astype(jnp.bfloat16)

        grad_rows = grad_blk.reshape(tokens, d_local)
        grad_hidden, grad_w_out = matmul_bwd(hidden, w_out, grad_rows)
        gelu_back = jax.vjp(gelu_tanh, pre_act)[1]
        grad_pre = gelu_back(grad_hidden.astype(jnp.bfloat16).astype(jnp.float32))[0]
        grad_normed2, grad_w_in = matmul_bwd(normed2, w_in, grad_pre.astype(jnp.bfloat16))
        ln2_grad, grad_ln2_scale, grad_ln2_shift = layer_norm_bwd(grad_normed2.astype(jnp.bfloat16), ln2_hat, ln2_inv, ln2_scale, feat_width)
        grad_resid = (grad_rows.astype(jnp.float32) + ln2_grad).astype(jnp.bfloat16)
        grad_attn, grad_w_o = matmul_bwd(attn_rows, w_o, grad_resid)
        grad_items = grad_attn.astype(jnp.bfloat16).reshape(seq_count, seq_len, heads_local, head_dim).transpose(0, 2, 1, 3).reshape(seq_count * heads_local, seq_len, head_dim)
        grad_heads = lax.map(attend_item_back, (head_items, grad_items))
        grad_qkv = grad_heads.reshape(seq_count, heads_local, 3, seq_len, head_dim).transpose(0, 3, 1, 2, 4).reshape(tokens, heads_local * qkv_width)
        grad_normed1, grad_w_qkv = matmul_bwd(normed1, w_qkv, grad_qkv)
        ln1_grad, grad_ln1_scale, grad_ln1_shift = layer_norm_bwd(grad_normed1.astype(jnp.bfloat16), ln1_hat, ln1_inv, ln1_scale, feat_width)
        grad_x = (grad_resid.astype(jnp.float32) + ln1_grad).astype(jnp.bfloat16)
        return (out_rows.reshape(x_blk.shape), grad_x.reshape(x_blk.shape), grad_ln1_scale, grad_ln1_shift, grad_w_qkv, bias_grad(grad_qkv).reshape(heads_local, qkv_width), grad_w_o, bias_grad(grad_resid), grad_ln2_scale, grad_ln2_shift, grad_w_in, bias_grad(grad_pre), grad_w_out, bias_grad(grad_rows))

    return jax.shard_map(layer_block, mesh=mesh,
                         in_specs=(act_spec, vec_spec, vec_spec, mat_spec, head_spec, mat_spec, vec_spec, vec_spec, vec_spec, mat_spec, vec_spec, mat_spec, vec_spec, act_spec),
                         out_specs=(act_spec, act_spec, gvec_spec, gvec_spec, gmat_spec, ghead_spec, gmat_spec, gvec_spec, gvec_spec, gvec_spec, gmat_spec, gvec_spec, gmat_spec, gvec_spec),
                         check_vma=False)
```

profile of v0, /device:TPU:0, one launch (start us, length us, event | category | flops | bytes accessed | tf_op | source)
XLA Modules:
  0.0 1853.1 jit_solution(15029833194049019946)
XLA Ops:
  9.1 13.7 psum.84
  26.3 59.5 %all-gather.9.cloned.1.call-done = bf16[768,2048]{0,1:T(8,128)(2,1)} async-done(((bf16[768,512]{0,1:T(8,128)(2,1)}), bf16[768,2048]{0,1:T(8,128)(2,1)}) %all-gather.9.cloned.1.call-update) | async-done | bytes 3145744 | tf_op jit(solution)/shard_map/all_gather | solution.py:58
  85.8 46.8 %all-gather.11.cloned.1.call-done = bf16[2048,1536]{1,0:T(8,128)(2,1)} async-done(((bf16[512,1536]{1,0:T(8,128)(2,1)}), bf16[2048,1536]{1,0:T(8,128)(2,1)}) %all-gather.11.cloned.1.call-update) | async-done | bytes 6291472 | tf_op jit(solution)/shard_map/all_gather | solution.py:54
  132.6 9.3 add_convert_fusion
  141.9 2.8 copy.38
  144.7 4.0 copy.39
  148.7 32.3 %while.20 = (s32[]{:T(128)}, bf16[8,768,64]{1,2,0:T(8,128)(2,1)}, bf16[8,3,768,64]{3,2,1,0:T(8,128)(2,1)}, s32[]{:T(128)}, s32[]{:T(128)}, /*index=5*/s32[]{}, s32[]{}) while((s32[]{:T(128)}, bf16[8,768,64]{1,2,0:T(8,128)(2,1)}, bf16[8,3,768,64]{3,2,1,0:T(8,128)(2,1)}, s32[]{:T(128)}, s32[]{:T(128)}, /*index=5*/s32[]{}, s32[]{}) %tuple.67), condition=%wide.region_6.7_spmd, body=%wide.region_3.6_spmd.sunk | while | flops 156350976 | bytes 7784557 | solution.py:97
  148.7 1.6 fusion.135
  150.6 2.1 fusion.137
  152.7 1.6 fusion.135
  154.6 2.1 fusion.137
  158.7 2.1 fusion.137
  162.7 2.1 fusion.137
  166.8 2.1 fusion.137
  170.8 2.1 fusion.137
  174.9 2.1 fusion.137
  177.0 1.6 fusion.135
  178.9 2.1 fusion.137
  182.3 61.7 %all-gather.13.cloned.1.call-done = bf16[768,2048]{0,1:T(8,128)(2,1)} async-done(((bf16[768,512]{0,1:T(8,128)(2,1)}), bf16[768,2048]{0,1:T(8,128)(2,1)}) %all-gather.13.cloned.1.call-update) | async-done | bytes 3145744 | tf_op jit(solution)/shard_map/all_gather | solution.py:58
  244.0 4.5 convert_reduce_fusion.1
  248.6 9.9 psum.85
  259.8 42.9 %all-gather.23.cloned.1.call-done = bf16[8192,512]{1,0:T(8,128)(2,1)} async-done(((bf16[2048,512]{1,0:T(8,128)(2,1)}), bf16[8192,512]{1,0:T(8,128)(2,1)}) %all-gather.23.cloned.1.call-update) | async-done | bytes 8388624 | tf_op jit(solution)/shard_map/all_gather | solution.py:54
  302.8 15.1 fusion.85
  318.4 44.3 %all-gather.19.cloned.1.call-done = bf16[2048,2048]{1,0:T(8,128)(2,1)} async-done(((bf16[512,2048]{1,0:T(8,128)(2,1)}), bf16[2048,2048]{1,0:T(8,128)(2,1)}) %all-gather.19.cloned.1.call-update) | async-done | bytes 8388624 | tf_op jit(solution)/shard_map/all_gather | solution.py:54
  362.7 64.9 %all-gather.17.cloned.1.call-done = bf16[768,2048]{0,1:T(8,128)(2,1)} async-done(((bf16[768,512]{0,1:T(8,128)(2,1)}), bf16[768,2048]{0,1:T(8,128)(2,1)}) %all-gather.17.cloned.1.call-update) | async-done | bytes 3145744 | tf_op jit(solution)/shard_map/all_gather | solution.py:58
  427.7 415.1 %reduce-scatter.9.cloned.1.call-done = f32[768,2048]{1,0:T(8,128)} async-done(((f32[768,8192]{1,0:T(8,128)}), f32[768,2048]{1,0:T(8,128)}) %reduce-scatter.9.cloned.1.call-update) | async-done | bytes 6291472 | tf_op jit(solution)/shard_map/reduce_scatter | solution.py:67
  842.8 17.7 fusion.89
  860.4 1.7 copy-done.24
  862.1 8.5 fusion.79
  871.0 111.5 %reduce-scatter.11.cloned.1.call-done = f32[768,512]{0,1:T(8,128)} async-done(((f32[768,2048]{0,1:T(8,128)}), f32[768,512]{0,1:T(8,128)}) %reduce-scatter.11.cloned.1.call-update) | async-done | bytes 1572880 | tf_op jit(solution)/shard_map/reduce_scatter | solution.py:67
  982.5 2.1 fusion.67
  984.6 11.6 psum.86
  997.8 4.4 fusion.93
  1003.0 5.7 fusion.95
  1008.8 12.5 fusion.77
  1021.5 89.7 %reduce-scatter.13.cloned.1.call-done = f32[768,512]{1,0:T(8,128)} async-done(((f32[768,2048]{1,0:T(8,128)}), f32[768,512]{1,0:T(8,128)}) %reduce-scatter.13.cloned.1.call-update) | async-done | bytes 1572880 | tf_op jit(solution)/shard_map/reduce_scatter | solution.py:67
  1113.9 71.8 %while.21 = (s32[]{:T(128)}, bf16[8,3,768,64]{2,3,1,0:T(8,128)(2,1)}, bf16[8,768,64]{1,2,0:T(8,128)(2,1)}, bf16[8,3,768,64]{3,2,1,0:T(8,128)(2,1)}, s32[]{:T(128)}, /*index=5*/s32[]{:T(128)}, s32[]{}, s32[]{}) while((s32[]{:T(128)}, bf16[8,3,768,64]{2,3,1,0:T(8,128)(2,1)}, bf16[8,768,64]{1,2,0:T(8,128)(2,1)}, ...), condition=%wide.region_20.21_spmd, body=%wide.region_16.0_spmd.sunk | while | flops 399065088 | bytes 19808392 | solution.py:114
  1117.2 1.6 fusion.144
  1126.2 1.6 fusion.144
  1135.2 1.6 fusion.144
  1144.2 1.6 fusion.144
  1153.1 1.6 fusion.144
  1162.1 1.6 fusion.144
  1171.1 1.6 fusion.144
  1180.0 1.6 fusion.144
  1185.8 9.6 fusion.96
  1195.4 1.6 copy-done.4
  1197.0 9.9 fusion.94
  1207.2 125.1 %all-gather.21.cloned.1.call-done = bf16[768,8192]{1,0:T(8,128)(2,1)} async-done(((bf16[768,2048]{1,0:T(8,128)(2,1)}), bf16[768,8192]{1,0:T(8,128)(2,1)}) %all-gather.21.cloned.1.call-update) | async-done | bytes 12582928 | tf_op jit(solution)/shard_map/all_gather | solution.py:58
  1332.3 15.1 fusion.83
  1348.5 12.1 fusion.81
  1360.5 2.4 copy.47
  1363.0 13.7 reduce-scatter.19.cloned.1.call-done
  1376.7 2.1 convert_element_type.131
  1379.2 124.3 %reduce-scatter.21.cloned.1.call-done = f32[512,2048]{1,0:T(8,128)} async-done(((f32[2048,2048]{1,0:T(8,128)}), f32[512,2048]{1,0:T(8,128)}) %reduce-scatter.21.cloned.1.call-update) | async-done | bytes 4194320 | tf_op jit(solution)/shard_map/reduce_scatter | solution.py:69
  1503.6 3.8 convert_element_type.132
  1507.4 108.9 %reduce-scatter.15.cloned.1.call-done = f32[768,512]{0,1:T(8,128)} async-done(((f32[768,2048]{0,1:T(8,128)}), f32[768,512]{0,1:T(8,128)}) %reduce-scatter.15.cloned.1.call-update) | async-done | bytes 1572880 | tf_op jit(solution)/shard_map/reduce_scatter | solution.py:67
  1616.3 2.1 fusion.68
  1618.5 11.4 psum.87
  1631.7 10.9 all-reduce
  1642.6 73.1 %reduce-scatter.17.cloned.1.call-done = f32[512,1536]{1,0:T(8,128)} async-done(((f32[2048,1536]{1,0:T(8,128)}), f32[512,1536]{1,0:T(8,128)}) %reduce-scatter.17.cloned.1.call-update) | async-done | bytes 3145744 | tf_op jit(solution)/shard_map/reduce_scatter | solution.py:69
  1715.6 3.2 convert_element_type.129
  1718.8 123.6 %reduce-scatter.23.cloned.1.call-done = f32[2048,512]{1,0:T(8,128)} async-done(((f32[8192,512]{1,0:T(8,128)}), f32[2048,512]{1,0:T(8,128)}) %reduce-scatter.23.cloned.1.call-update) | async-done | bytes 4194320 | tf_op jit(solution)/shard_map/reduce_scatter | solution.py:69
  1842.4 3.8 convert_element_type.133
  (202 shorter events, 86.9 us)
Async XLA Ops:
  7.2 16.3 copy-start.18
  7.2 16.2 copy-start.14
  7.2 78.6 %all-gather.9.cloned.1.call-start = ((), (), s32[]{:S(2)}) async-start(), calls=%async_computation.8 | async-start | bytes 3932160 | tf_op jit(solution)/shard_map/all_gather | solution.py:58
  8.7 235.3 %copy-start = (bf16[1,768,512]{1,2,0:T(8,128)(2,1)}, bf16[1,768,512]{1,2,0:T(8,128)(2,1)S(1)}, u32[]{:S(2)}) copy-start(bf16[1,768,512]{1,2,0:T(8,128)(2,1)S(1)} %copy.37) | copy-start | bytes 2359300
  9.0 17.2 copy-start.17
  22.8 0.6 copy-start.9
  22.8 0.6 copy-start.11
  24.6 108.0 %all-gather.11.cloned.1.call-start = ((), (), s32[]{:S(2)}) async-start(), calls=%async_computation.9 | async-start | bytes 7864320 | tf_op jit(solution)/shard_map/all_gather | solution.py:54
  25.4 156.9 %all-gather.15.cloned.1.call-start = ((), (), s32[]{:S(2)}) async-start(), calls=%async_computation.11 | async-start | bytes 2621440 | tf_op jit(solution)/shard_map/all_gather | solution.py:54
  26.1 217.8 %all-gather.13.cloned.1.call-start = ((), (), s32[]{:S(2)}) async-start(), calls=%async_computation.10 | async-start | bytes 3932160 | tf_op jit(solution)/shard_map/all_gather | solution.py:58
  181.0 63.0 %copy-start.22 = (f32[512]{0:T(512)S(1)}, f32[512]{0:T(512)}, u32[]{:S(2)}) copy-start(f32[512]{0:T(512)} %param.24) | copy-start | bytes 6148
  181.0 121.7 %all-gather.23.cloned.1.call-start = ((), (), s32[]{:S(2)}) async-start(), calls=%async_computation.15 | async-start | bytes 10485760 | tf_op jit(solution)/shard_map/all_gather | solution.py:54
  181.6 181.1 %all-gather.19.cloned.1.call-start = ((), (), s32[]{:S(2)}) async-start(), calls=%async_computation.13 | async-start | bytes 10485760 | tf_op jit(solution)/shard_map/all_gather | solution.py:54
  182.2 76.3 %copy-start.13 = (f32[512]{0:T(512)S(1)}, f32[512]{0:T(512)}, u32[]{:S(2)}) copy-start(f32[512]{0:T(512)} %param.25) | copy-start | bytes 6148
  182.2 76.3 %copy-start.19 = (f32[512]{0:T(512)S(1)}, f32[512]{0:T(512)}, u32[]{:S(2)}) copy-start(f32[512]{0:T(512)} %param.26) | copy-start | bytes 6148
  182.2 245.4 %all-gather.17.cloned.1.call-start = ((), (), s32[]{:S(2)}) async-start(), calls=%async_computation.12 | async-start | bytes 3932160 | tf_op jit(solution)/shard_map/all_gather | solution.py:58
  248.5 747.7 %copy-start.2 = (bf16[768,512]{0,1:T(8,128)(2,1)}, bf16[768,512]{0,1:T(8,128)(2,1)S(1)}, u32[]{:S(2)}) copy-start(bf16[768,512]{0,1:T(8,128)(2,1)S(1)} %get-tuple-element.144) | copy-start | bytes 2359300
  248.5 54.2 %copy-start.7 = (bf16[1,768,512]{2,1,0:T(8,128)(2,1)S(1)}, bf16[1,768,512]{2,1,0:T(8,128)(2,1)}, u32[]{:S(2)}) copy-start(bf16[1,768,512]{2,1,0:T(8,128)(2,1)} %param.31) | copy-start | bytes 2359300
  259.8 583.0 %reduce-scatter.9.cloned.1.call-start = ((), (), s32[]{:S(2)}) async-start(), calls=%async_computation.16 | async-start | bytes 31457280 | tf_op jit(solution)/shard_map/reduce_scatter | solution.py:67
  317.8 524.9 %copy-start.21 = (f32[2048]{0:T(1024)S(1)}, f32[2048]{0:T(1024)}, u32[]{:S(2)}) copy-start(f32[2048]{0:T(1024)} %param.28) | copy-start | bytes 24580
  317.9 664.6 %reduce-scatter.11.cloned.1.call-start = ((), (), s32[]{:S(2)}) async-start(), calls=%async_computation.17 | async-start | bytes 7864320 | tf_op jit(solution)/shard_map/reduce_scatter | solution.py:67
  842.8 19.4 %copy-start.20 = (bf16[2048,2048]{1,0:T(8,128)(2,1)S(1)}, bf16[2048,2048]{1,0:T(8,128)(2,1)}, u32[]{:S(2)}) copy-start(bf16[2048,2048]{1,0:T(8,128)(2,1)} %all-gather.19.cloned.1.call-done) | copy-start | bytes 25165828
  860.4 1.7 copy-start.24
  870.7 240.6 %reduce-scatter.13.cloned.1.call-start = ((), (), s32[]{:S(2)}) async-start(), calls=%async_computation.18 | async-start | bytes 7864320 | tf_op jit(solution)/shard_map/reduce_scatter | solution.py:67
  996.2 1.6 copy-start.6
  1002.2 330.1 %all-gather.21.cloned.1.call-start = ((), (), s32[]{:S(2)}) async-start(), calls=%async_computation.14 | async-start | bytes 15728640 | tf_op jit(solution)/shard_map/all_gather | solution.py:58
  1002.9 373.7 %reduce-scatter.19.cloned.1.call-start = ((), (), s32[]{:S(2)}) async-start(), calls=%async_computation.21 | async-start | bytes 5242880 | tf_op jit(solution)/shard_map/reduce_scatter | solution.py:69
  1008.7 494.8 %reduce-scatter.21.cloned.1.call-start = ((), (), s32[]{:S(2)}) async-start(), calls=%async_computation.22 | async-start | bytes 20971520 | tf_op jit(solution)/shard_map/reduce_scatter | solution.py:69
  1021.3 595.0 %reduce-scatter.15.cloned.1.call-start = ((), (), s32[]{:S(2)}) async-start(), calls=%async_computation.19 | async-start | bytes 7864320 | tf_op jit(solution)/shard_map/reduce_scatter | solution.py:67
  1195.3 1.7 copy-start.4
  1195.4 520.3 %reduce-scatter.17.cloned.1.call-start = ((), (), s32[]{:S(2)}) async-start(), calls=%async_computation.20 | async-start | bytes 15728640 | tf_op jit(solution)/shard_map/reduce_scatter | solution.py:69
  1206.9 125.4 %copy-start.8 = (bf16[1,768,512]{2,1,0:T(8,128)(2,1)S(1)}, bf16[1,768,512]{2,1,0:T(8,128)(2,1)}, u32[]{:S(2)}) copy-start(bf16[1,768,512]{2,1,0:T(8,128)(2,1)} %param.31) | copy-start | bytes 2359300
  1206.9 635.5 %reduce-scatter.23.cloned.1.call-start = ((), (), s32[]{:S(2)}) async-start(), calls=%async_computation.23 | async-start | bytes 20971520 | tf_op jit(solution)/shard_map/reduce_scatter | solution.py:69
  1347.3 1.1 copy-start.3
  1347.3 1.1 copy-start.23
  1360.5 18.2 copy-start.5
  1379.2 237.1 %copy-start.1 = (bf16[1,768,512]{1,2,0:T(8,128)(2,1)S(1)}, bf16[1,768,512]{1,2,0:T(8,128)(2,1)}, u32[]{:S(2)}) copy-start(bf16[1,768,512]{1,2,0:T(8,128)(2,1)} %copy-done) | copy-start | bytes 2359300
  1379.2 237.1 %copy-start.10 = (f32[768]{0:T(1024)S(1)}, f32[768]{0:T(1024)}, u32[]{:S(2)}) copy-start(f32[768]{0:T(1024)} %copy-done.9) | copy-start | bytes 9220
  1379.2 237.1 %copy-start.12 = (f32[768]{0:T(1024)S(1)}, f32[768]{0:T(1024)}, u32[]{:S(2)}) copy-start(f32[768]{0:T(1024)} %copy-done.11) | copy-start | bytes 9220
  1379.2 237.1 %copy-start.15 = (f32[512]{0:T(512)S(1)}, f32[512]{0:T(512)}, u32[]{:S(2)}) copy-start(f32[512]{0:T(512)} %param.19) | copy-start | bytes 6148
  1629.9 1.8 copy-start.16
Sparse Core Ops, SparseCore 0:
  24.8 60.9 all-gather.8
  87.3 45.2 all-gather.10
  134.2 22.3 all-gather.14
  181.2 62.7 all-gather.12
  245.4 57.3 all-gather.22
  304.2 58.4 all-gather.18
  364.8 62.7 all-gather.16
  430.0 412.6 reduce-scatter.8
  870.8 111.6 reduce-scatter.10
  1002.3 108.9 reduce-scatter.12
  1112.9 219.3 all-gather.20
  1334.6 41.9 reduce-scatter.18
  1379.3 124.2 reduce-scatter.20
  1505.7 110.5 reduce-scatter.14
  1618.8 96.8 reduce-scatter.16
  1718.1 124.2 reduce-scatter.22
where the time goes:
time: 1860 us; the launch traced here: 1850 us
  waiting for transfers between devices  1510 us (81%)
  matrix products  212 us (11%)
  blocking collectives  57.5 us (3%)
  other arithmetic  39.2 us (2%)
  local copies, waits for them, and re-layouts  19 us (1%)
    reduce_scatter x4, waiting for transfers between devices, matmul_bwd(): lax.psum_scatter(part_act, 'col', scatter_dimension=1, tiled=True)  725 us
    reduce_scatter x4, waiting for transfers between devices, matmul_bwd(): grad_w = lax.psum_scatter(part_w, 'row', scatter_dimension=0, tiled=True)  335 us
    all_gather x4, waiting for transfers between devices, gather_features(): return lax.all_gather(act_blk, 'col', axis=1, tiled=True)  311 us
    all_gather x4, waiting for transfers between devices, gather_weight(): return lax.all_gather(w_blk, 'row', axis=0, tiled=True)  134 us
    dot_general x32, matrix products, attend_one(): lax.dot_general(query_rows, key_rows, (((1,), (1,)), ((), ())), preferred...  46.6 us
    dot_general x4, matrix products, matmul_fwd(): jnp.dot(gather_features(act_blk), gather_weight(w_blk), preferred_element...  43.5 us
    dot_general x4, matrix products, matmul_bwd(): lax.dot_general(gather_features(act_blk), grad_blk, (((0,), (0,)), ((), (...  43.1 us
    dot_general x24, matrix products, attend_one(): jnp.dot(attn_probs.astype(jnp.bfloat16), value_rows, preferred_element_ty...  41.4 us
  transfers between devices with their start and end apart: 16, of which 15 were waited for; matrix products, arithmetic and copies ran while one was open for 12% of the time, Pallas kernels for 0%

commit v1 on v0

v1 whole, which is shorter than its diff:
```python
import jax
import jax.numpy as jnp
from jax import lax
from jax.sharding import PartitionSpec as P

LN_EPS = 1e-5
BF16 = jnp.bfloat16
F32 = jnp.float32


def gelu_tanh(pre_act):
    return jax.nn.gelu(pre_act, approximate=True)


def attend_one(query_rows, key_rows, value_rows):
    seq_len, head_dim = query_rows.shape
    scores = lax.dot_general(query_rows, key_rows, (((1,), (1,)), ((), ())), preferred_element_type=jnp.float32)
    query_pos = lax.broadcasted_iota(jnp.int32, (seq_len, 1), 0)
    key_pos = lax.broadcasted_iota(jnp.int32, (1, seq_len), 1)
    attn_probs = jax.nn.softmax(jnp.where(key_pos <= query_pos, scores * head_dim ** -0.5, -1e30), axis=-1)
    return jnp.dot(attn_probs.astype(jnp.bfloat16), value_rows, preferred_element_type=jnp.float32).astype(jnp.bfloat16)


def attend_item(head_item):
    return attend_one(head_item[0], head_item[1], head_item[2])


def attend_item_back(item_pair):
    head_item, grad_item = item_pair
    pullback = jax.vjp(attend_one, head_item[0], head_item[1], head_item[2])[1]
    return jnp.stack(pullback(grad_item))


def dot_nn(lhs, rhs):
    return jnp.dot(lhs, rhs, preferred_element_type=F32)


def dot_nt(lhs, rhs):
    return lax.dot_general(lhs, rhs, (((1,), (1,)), ((), ())), preferred_element_type=F32)


def dot_tn(lhs, rhs):
    return lax.dot_general(lhs, rhs, (((0,), (0,)), ((), ())), preferred_element_type=F32)


def norm_stats(act_f32, width):
    mean_val = jnp.sum(act_f32, axis=-1, keepdims=True) / width
    mean_sq = jnp.sum(act_f32 * act_f32, axis=-1, keepdims=True) / width
    return mean_val, lax.rsqrt(mean_sq - mean_val * mean_val + LN_EPS)


def solution(mesh):
    n_row, n_col = mesh.shape['row'], mesh.shape['col']
    act_spec = P(('dp', 'row'), None, 'col')
    vec_spec = P('col')
    mat_spec = P('row', 'col')
    head_spec = P('col', None)
    gvec_spec = P(('dp', 'col'))
    gmat_spec = P(('dp', 'row'), 'col')
    ghead_spec = P(('dp', 'col'), None)

    def flip_row(val, bits):
        return lax.ppermute(val, 'row', [(src, src ^ bits) for src in range(n_row)])

    def shift_col(val, step):
        return lax.ppermute(val, 'col', [(src, (src + step) % n_col) for src in range(n_col)])

    def swap_axes(val):
        pairs = [(r * n_col + c, c * n_col + r) for r in range(n_row) for c in range(n_col)]
        return lax.ppermute(val, ('col', 'row'), pairs)

    def gather_row(w_blk, axis):
        row = lax.axis_index('row')
        far = flip_row(w_blk, 2)
        mate = flip_row(w_blk, 1)
        far_mate = flip_row(far, 1)
        size = w_blk.shape[axis]
        shape = list(w_blk.shape)
        shape[axis] = n_row * size
        full = jnp.zeros(shape, w_blk.dtype)
        for bits, part in ((0, w_blk), (1, mate), (2, far), (3, far_mate)):
            full = lax.dynamic_update_slice_in_dim(full, part, (row ^ bits) * size, axis)
        return full

    def scatter_row(make_part):
        row = lax.axis_index('row')
        sent_a, sent_b = make_part(row ^ 3), make_part(row ^ 1)
        got_a, got_b = flip_row(sent_a, 1), flip_row(sent_b, 1)
        far = flip_row(make_part(row ^ 2) + got_a, 2)
        return (make_part(row) + got_b + far).astype(BF16)

    def sum_row(val):
        val = val + flip_row(val, 1)
        return val + flip_row(val, 2)

    def layer_block(x_blk, ln1_scale, ln1_shift, w_qkv, b_qkv, w_o, b_o, ln2_scale, ln2_shift, w_in, b_in, w_out, b_out, grad_blk):
        seq_count, seq_len, d_local = x_blk.shape
        tokens = seq_count * seq_len
        heads_local, qkv_width = b_qkv.shape
        head_dim = qkv_width // 3
        width = d_local * n_col
        col = lax.axis_index('col')
        x_rows = x_blk.reshape(tokens, d_local)
        grad_rows = grad_blk.reshape(tokens, d_local)

        def col_block(val, axis, index, size):
            return lax.dynamic_slice_in_dim(val, index * size, size, axis)

        vecs = lax.all_gather(jnp.stack([ln1_scale, ln1_shift, b_o, ln2_scale, ln2_shift]), 'col', axis=1, tiled=True)
        s1, t1, bo, s2, t2 = [vecs[i:i + 1] for i in range(5)]

        x_full = lax.all_gather(x_rows, 'col', axis=1, tiled=True)
        wq = gather_row(w_qkv, 0)
        x32 = x_full.astype(F32)
        mean1, inv1 = norm_stats(x32, width)
        h1 = ((x32 - mean1) * inv1 * s1 + t1).astype(BF16)
        qkv_rows = (dot_nn(h1, wq) + b_qkv.reshape(heads_local * qkv_width)).astype(BF16)
        head_items = qkv_rows.reshape(seq_count, seq_len, heads_local, 3, head_dim).transpose(0, 2, 3, 1, 4).reshape(seq_count * heads_local, 3, seq_len, head_dim)
        attn_items = lax.map(attend_item, head_items)
        attn_rows = attn_items.reshape(seq_count, heads_local, seq_len, head_dim).transpose(0, 2, 1, 3).reshape(tokens, d_local)
        attn_full = lax.all_gather(attn_rows, 'col', axis=1, tiled=True)

        wo = gather_row(lax.all_gather(w_o, 'col', axis=1, tiled=True), 0)
        wi = gather_row(w_in, 0)
        wt = gather_row(swap_axes(w_out), 1)
        g_full = lax.all_gather(grad_rows, 'col', axis=1, tiled=True)

        r1 = (x32 + dot_nn(attn_full, wo) + bo).astype(BF16)
        r32 = r1.astype(F32)
        mean2, inv2 = norm_stats(r32, width)
        h2 = ((r32 - mean2) * inv2 * s2 + t2).astype(BF16)
        pre_act = dot_nn(h2, wi) + b_in
        hidden, gelu_back = jax.vjp(gelu_tanh, pre_act)
        hidden = hidden.astype(BF16)

        grad_hidden = dot_nt(g_full, wt).astype(BF16)
        grad_pre = gelu_back(grad_hidden.astype(F32))[0].astype(BF16)
        tok_local = tokens // n_col
        gn2 = lax.psum_scatter(dot_nt(grad_pre, wi), 'col', scatter_dimension=0, tiled=True).astype(BF16).astype(F32)
        r_tok = col_block(r1, 0, col, tok_local).astype(F32)
        mean_t, inv_t = col_block(mean2, 0, col, tok_local), col_block(inv2, 0, col, tok_local)
        hat_t = (r_tok - mean_t) * inv_t
        gs2 = jnp.stack([jnp.sum(gn2 * hat_t, axis=0), jnp.sum(gn2, axis=0)])
        ghat = gn2 * s2
        gin = inv_t * (ghat - jnp.mean(ghat, axis=-1, keepdims=True) - hat_t * jnp.mean(ghat * hat_t, axis=-1, keepdims=True))
        gr_tok = (col_block(g_full, 0, col, tok_local).astype(F32) + gin).astype(BF16)
        gr = lax.all_gather(gr_tok, 'col', axis=0, tiled=True)
        gr_mine = col_block(gr, 1, col, d_local)

        grad_attn = dot_nt(gr, col_block(wo, 0, col, d_local)).astype(BF16)
        grad_items = grad_attn.reshape(seq_count, seq_len, heads_local, head_dim).transpose(0, 2, 1, 3).reshape(seq_count * heads_local, seq_len, head_dim)
        grad_heads = lax.map(attend_item_back, (head_items, grad_items))
        grad_qkv = grad_heads.reshape(seq_count, heads_local, 3, seq_len, head_dim).transpose(0, 3, 1, 2, 4).reshape(tokens, heads_local * qkv_width)

        hidden_late, _ = lax.optimization_barrier((hidden, gr))
        out_part = lax.psum_scatter(dot_nn(hidden_late, wt), 'col', scatter_dimension=1, tiled=True)
        out_rows = (col_block(r1, 1, col, d_local).astype(F32) + out_part + b_out).astype(BF16)

        gn1 = lax.psum_scatter(dot_nt(grad_qkv, wq), 'col', scatter_dimension=1, tiled=True).astype(BF16).astype(F32)
        hat1 = (x_rows.astype(F32) - mean1) * inv1
        ghat1 = gn1 * ln1_scale
        sums = jnp.stack([jnp.sum(ghat1, axis=-1), jnp.sum(ghat1 * hat1, axis=-1)])
        sums = (sums + shift_col(sums, 1) + shift_col(sums, 2) + shift_col(sums, 3)) / width
        gx = gr_mine.astype(F32) + inv1 * (ghat1 - sums[0][:, None] - hat1 * sums[1][:, None])
        grad_x = gx.astype(BF16)

        grad_wout = swap_axes(scatter_row(lambda j: dot_tn(hidden, col_block(g_full, 1, j, d_local))))
        grad_win = scatter_row(lambda j: dot_tn(col_block(h2, 1, j, width // n_row), grad_pre))
        grad_wo = scatter_row(lambda j: dot_tn(col_block(attn_full, 1, j, width // n_row), gr_mine))
        grad_wqkv = scatter_row(lambda j: dot_tn(col_block(h1, 1, j, width // n_row), grad_qkv))

        def tok_sum(val):
            return jnp.sum(val.astype(F32), axis=0)

        ln2_part = col_block(gs2, 1, col, d_local)
        for step in range(1, n_col):
            ln2_part = ln2_part + shift_col(col_block(gs2, 1, (col + step) % n_col, d_local), step)
        early = sum_row(jnp.concatenate([ln2_part.reshape(-1), tok_sum(grad_rows), tok_sum(gr_mine), tok_sum(grad_pre)]))
        gl2s, gl2t, gbout, gbo, gbin = jnp.split(early, [d_local * k for k in range(1, 5)])
        gbqkv = sum_row(tok_sum(grad_qkv))
        late = sum_row(jnp.stack([jnp.sum(gn1 * hat1, axis=0), jnp.sum(gn1, axis=0)]))
        return (out_rows.reshape(x_blk.shape), grad_x.reshape(x_blk.shape), late[0], late[1], grad_wqkv, gbqkv.reshape(heads_local, qkv_width), grad_wo, gbo, gl2s, gl2t, grad_win, gbin, grad_wout, gbout)

    return jax.shard_map(layer_block, mesh=mesh,
                         in_specs=(act_spec, vec_spec, vec_spec, mat_spec, head_spec, mat_spec, vec_spec, vec_spec, vec_spec, mat_spec, vec_spec, mat_spec, vec_spec, act_spec),
                         out_specs=(act_spec, act_spec, gvec_spec, gvec_spec, gmat_spec, ghead_spec, gmat_spec, gvec_spec, gvec_spec, gvec_spec, gmat_spec, gvec_spec, gmat_spec, gvec_spec),
                         check_vma=False)
```

time: 1860 us -> 1120 us (0.60)
  waiting for transfers between devices: 1510 us -> 524 us
  starting transfers between devices: 1.58 us -> 199 us
  local copies, waits for them, and re-layouts: 19 us -> 72.8 us
  blocking collectives: 57.5 us -> 14 us
    reduce_scatter x8 -> x3, waiting for transfers between devices: 1060 us -> 145 us  [the longest x1 145 us: layer_block(): lax.psum_scatter(dot_nt(grad_pre, wi), 'col', scatter_dimension=0, tiled=...]
    all_gather x8 -> x5, waiting for transfers between devices: 445 us -> 69.1 us  [the longest x1 63.6 us: layer_block(): gr = lax.all_gather(gr_tok, 'col', axis=0, tiled=True)]
    ppermute x0 -> x38, waiting for transfers between devices: none -> 309 us  [the longest x30 264 us: flip_row(): return lax.ppermute(val, 'row', [(src, src ^ bits) for src in range(n_row)])]
    ppermute x0 -> x38, starting transfers between devices: none -> 199 us  [the longest x30 158 us: flip_row(): return lax.ppermute(val, 'row', [(src, src ^ bits) for src in range(n_row)])]
    psum x5 -> x0, blocking collectives: 57.5 us -> none  [the longest x2 23.6 us: layer_norm_fwd(): ln_stats = lax.psum(ln_stats, 'col') / feat_width]
    dynamic_update_slice x0 -> x16, local copies, waits for them, and re-layouts: none -> 32.6 us  [gather_row(): lax.dynamic_update_slice_in_dim(full, part, (row ^ bits) * size, axis)]
    dot_general x12 -> x24, matrix products: 124 us -> 146 us  [the longest x16 60.5 us: dot_tn(): lax.dot_general(lhs, rhs, (((0,), (0,)), ((), ())), preferred_element_typ...]
  transfers between devices with their start and end apart: 16 -> 46, of which waited for: 15 -> 13; matrix products, arithmetic and copies ran while one was open for 12% -> 19% of each run, Pallas kernels for 0% -> 0%
where the time goes in v1:
time: 1120 us; the launch traced here: 1100 us
  waiting for transfers between devices  524 us (47%)
  matrix products  229 us (20%)
  starting transfers between devices  199 us (18%)
  local copies, waits for them, and re-layouts  72.8 us (6%)
  other arithmetic  48.9 us (4%)
  between operations  15.1 us (1%)
  blocking collectives  14 us (1%)
    ppermute x30, waiting for transfers between devices, flip_row(): return lax.ppermute(val, 'row', [(src, src ^ bits) for src in range(n_row)])  264 us
    ppermute x30, starting transfers between devices, flip_row(): return lax.ppermute(val, 'row', [(src, src ^ bits) for src in range(n_row)])  158 us
    reduce_scatter x1, waiting for transfers between devices, layer_block(): lax.psum_scatter(dot_nt(grad_pre, wi), 'col', scatter_dimension=0, tiled=...  145 us
    all_gather x1, waiting for transfers between devices, layer_block(): gr = lax.all_gather(gr_tok, 'col', axis=0, tiled=True)  63.6 us
    dot_general x16, matrix products, dot_tn(): lax.dot_general(lhs, rhs, (((0,), (0,)), ((), ())), preferred_element_typ...  60.5 us
    dot_general x32, matrix products, attend_one(): lax.dot_general(query_rows, key_rows, (((1,), (1,)), ((), ())), preferred...  46.6 us
    ppermute x6, waiting for transfers between devices, shift_col(): lax.ppermute(val, 'col', [(src, (src + step) % n_col) for src in range(n_...  45.4 us
    dot_general x4, matrix products, dot_nn(): return jnp.dot(lhs, rhs, preferred_element_type=F32)  43.7 us
  transfers between devices with their start and end apart: 46, of which 13 were waited for; matrix products, arithmetic and copies ran while one was open for 19% of the time, Pallas kernels for 0%

profile of v1, /device:TPU:0, one launch (start us, length us, event | category | flops | bytes accessed | tf_op | source)
XLA Modules:
  0.0 1104.0 jit_solution(12568538505485170077)
XLA Ops:
  8.0 3.1 collective-permute-start.1
  11.1 34.4 %collective-permute-done.1 = bf16[512,1536]{1,0:T(8,128)(2,1)S(1)} collective-permute-done((bf16[512,1536]{1,0:T(8,128)(2,1)}, bf16[512,1536]{1,0:T(8,128)(2,1)S(1)}, u32[]{:S(2)}, u32[]{:S(2)}) %collective-permute-start.1) | collective-permute-done | bytes 1572896 | tf_op jit(solution)/shard_map/ppermute | solution.py:63
  47.1 14.0 %all_gather.19 = f32[5,2048]{1,0:T(8,128)S(1)} all-gather(f32[5,512]{1,0:T(8,128)S(1)} %stack.62), channel_id=1, replica_groups=mesh['dp'=2,'col'=4,'row'=4] {'col'}, dimensions={1}, use_global_device_ids=true | all-gather | bytes 51200 | tf_op jit(solution)/shard_map/all_gather | solution.py:109
  61.1 3.1 broadcast_in_dim.46
  65.6 2.7 constant_dynamic-update-slice_fusion.14
  70.8 5.5 all-gather.14.cloned.1.call-done
  76.3 2.5 convert_reduce_fusion.1
  82.7 9.0 add_convert_fusion
  91.7 2.8 copy.30
  94.6 4.0 copy.31
  98.6 27.2 %while.20 = (s32[]{:T(128)}, bf16[8,768,64]{1,2,0:T(8,128)(2,1)S(1)}, bf16[8,3,768,64]{3,2,1,0:T(8,128)(2,1)}, s32[]{:T(128)}, s32[]{:T(128)}, /*index=5*/s32[]{}, s32[]{}) while((s32[]{:T(128)}, bf16[8,768,64]{1,2,0:T(8,128)(2,1)S(1)}, bf16[8,3,768,64]{3,2,1,0:T(8,128)(2,1)}, s32[]{:T(128)}, s32[]{:T(128)}, /*index=5*/s32[]{}, s32[]{}) %tuple.101), condition=%wide.region_5.6_spmd, body=%wide.region_2.5_spmd.sunk | while | flops 156350976 | bytes 7786605 | solution.py:119
  126.7 17.2 %collective-permute-start.9 = (bf16[2048,512]{1,0:T(8,128)(2,1)}, bf16[2048,512]{1,0:T(8,128)(2,1)}, u32[]{:S(2)}, u32[]{:S(2)}) collective-permute-start(bf16[2048,512]{1,0:T(8,128)(2,1)} %param.29), channel_id=1, source_target_pairs={{0,0},{1,4},{2,8},{3,12},{4,1},{5,5},{6,9},{7,13},{8,2},{9,6},{10,... | collective-permute-start | bytes 6291464 | tf_op jit(solution)/shard_map/ppermute | solution.py:70
  143.9 128.4 %collective-permute-start.11 = (bf16[2048,512]{1,0:T(8,128)(2,1)}, bf16[2048,512]{1,0:T(8,128)(2,1)}, u32[]{:S(2)}, u32[]{:S(2)}) collective-permute-start(bf16[2048,512]{1,0:T(8,128)(2,1)} %collective-permute-done.9), channel_id=1, source_target_pairs={{0,2},{1,3},{2,0},{3,1},{4,6},{5,7},{6,4},{7,5},{8,10},{9,11},{10,... | collective-permute-start | bytes 6291464 | tf_op jit(solution)/shard_map/ppermute | solution.py:63
  276.7 26.4 %collective-permute-done.11 = bf16[2048,512]{1,0:T(8,128)(2,1)} collective-permute-done((bf16[2048,512]{1,0:T(8,128)(2,1)}, bf16[2048,512]{1,0:T(8,128)(2,1)}, u32[]{:S(2)}, u32[]{:S(2)}) %collective-permute-start.11) | collective-permute-done | bytes 2097184 | tf_op jit(solution)/shard_map/ppermute | solution.py:63
  304.9 20.6 %collective-permute-done.4 = bf16[512,2048]{1,0:T(8,128)(2,1)} collective-permute-done((bf16[512,2048]{1,0:T(8,128)(2,1)}, bf16[512,2048]{1,0:T(8,128)(2,1)}, u32[]{:S(2)}, u32[]{:S(2)}) %collective-permute-start.4) | collective-permute-done | bytes 2097184 | tf_op jit(solution)/shard_map/ppermute | solution.py:63
  325.5 4.3 broadcast.126.clone.2
  329.8 3.1 constant_dynamic-update-slice_fusion.3
  332.9 4.3 broadcast.126.clone
  338.8 3.2 constant_dynamic-update-slice_fusion.2
  341.9 3.2 constant_dynamic-update-slice_fusion.1
  348.6 4.7 constant_dynamic-update-slice_fusion.9
  357.5 11.2 %convert_reduce_fusion = (f32[768]{0:T(1024)S(1)}, f32[768]{0:T(1024)S(1)}, bf16[768,2048]{1,0:T(8,128)(2,1)S(1)}) fusion(f32[2048]{0:T(1024)S(1)} %bitcast.246, bf16[768,2048]{0,1:T(8,128)(2,1)} %all-gather.8.cloned.1.call-done, bf16[2048,2048]{1,0:T(8,128)(2,1)} %constant_dynamic-update-slice_fusion.8, bf16[1,768,2048]{2,1,0:T(8,128)(2,1)S(1)} %copy-done.3), kind=kOutput, calls=%fused_computation.56 | convolution fusion | flops 6455031808 | bytes 17840128 | tf_op jit(solution)/shard_map/dot_general | solution.py:35
  372.1 12.5 %multiply_convert_fusion = (bf16[768,2048]{1,0:T(8,128)(2,1)}, f32[768,2048]{1,0:T(8,128)}) fusion(f32[2048]{0:T(1024)S(1)} %copy-done.28, bf16[768,2048]{1,0:T(8,128)(2,1)S(1)} %fusion.53, bf16[2048,2048]{1,0:T(8,128)(2,1)} %copy-done.10), kind=kOutput, calls=%fused_computation.89 | convolution fusion | flops 6458179584 | bytes 20979712 | tf_op jit(solution)/shard_map/dot_general | solution.py:35
  384.6 16.3 %convert_reduce_fusion.2 = (f32[2048]{0:T(1024)S(1)}, bf16[768,2048]{1,0:T(8,128)(2,1)S(1)}) fusion(f32[768,2048]{1,0:T(8,128)} %get-tuple-element.120, f32[2048]{0:T(1024)S(1)} %copy-done.28, bf16[2048,2048]{1,0:T(8,128)(2,1)} %constant_dynamic-update-slice_fusion, bf16[1,768,2048]{2,1,0:T(8,128)(2,1)} %all-gather.16.cloned.1.call-done), kind=kOutput, calls=%fused_computation.88 | convolution fusion | flops 6481770496 | bytes 20987904 | tf_op jit(solution)/shard_map/dot_general | solution.py:39
  402.5 11.0 fusion.152
  413.8 145.4 %reduce-scatter.4.cloned.1.call-done = f32[192,2048]{1,0:T(8,128)} async-done(((f32[768,2048]{1,0:T(8,128)}), f32[192,2048]{1,0:T(8,128)}) %reduce-scatter.4.cloned.1.call-update) | async-done | bytes 1572880 | tf_op jit(solution)/shard_map/reduce_scatter | solution.py:139
  559.2 2.2 fusion.80
  561.4 2.8 fusion.78
  564.3 63.6 %all-gather.12.cloned.1.call-done = bf16[768,2048]{1,0:T(8,128)(2,1)} async-done(((bf16[192,2048]{1,0:T(8,128)(2,1)}), bf16[768,2048]{1,0:T(8,128)(2,1)}) %all-gather.12.cloned.1.call-update) | async-done | bytes 3145744 | tf_op jit(solution)/shard_map/all_gather | solution.py:147
  627.9 4.4 fusion.84
  634.0 72.3 %while.21 = (s32[]{:T(128)}, bf16[8,3,768,64]{2,3,1,0:T(8,128)(2,1)}, bf16[8,768,64]{2,1,0:T(8,128)(2,1)}, bf16[8,3,768,64]{3,2,1,0:T(8,128)(2,1)}, s32[]{:T(128)}, /*index=5*/s32[]{:T(128)}, s32[]{}, s32[]{}) while((s32[]{:T(128)}, bf16[8,3,768,64]{2,3,1,0:T(8,128)(2,1)}, bf16[8,768,64]{2,1,0:T(8,128)(2,1)}, ...), condition=%wide.region_16.17_spmd, body=%wide.region_12.0_spmd.sunk | while | flops 399065088 | bytes 20005000 | solution.py:152
  706.3 9.7 fusion.154
  717.9 4.9 fusion.91
  722.8 11.0 fusion.153
  735.6 3.2 fusion.102
  739.4 3.8 fusion.94
  743.3 4.3 convolution_add_fusion.2
  749.2 3.9 fusion.105
  753.3 3.2 fusion.115
  756.7 4.0 convolution_add_fusion.3
  761.3 3.9 fusion.96
  765.2 75.9 %collective-permute-done.36 = f32[2048,512]{1,0:T(8,128)S(1)} collective-permute-done((f32[2048,512]{1,0:T(8,128)S(1)}, f32[2048,512]{1,0:T(8,128)S(1)}, u32[]{:S(2)}, u32[]{:S(2)}) %collective-permute-start.36) | collective-permute-done | bytes 4194336 | tf_op jit(solution)/shard_map/ppermute | solution.py:63
  841.1 5.1 add_convert_fusion.1
  846.2 17.2 %collective-permute-start.37 = (bf16[2048,512]{1,0:T(8,128)(2,1)}, bf16[2048,512]{1,0:T(8,128)(2,1)}, u32[]{:S(2)}, u32[]{:S(2)}) collective-permute-start(bf16[2048,512]{1,0:T(8,128)(2,1)} %add_convert_fusion.1), channel_id=1, source_target_pairs={{0,0},{1,4},{2,8},{3,12},{4,1},{5,5},{6,9},{7,13},{8,2},{9,6},{10,... | collective-permute-start | bytes 6291464 | tf_op jit(solution)/shard_map/ppermute | solution.py:70
  863.4 3.1 fusion.118
  866.5 5.0 convolution_add_fusion
  871.5 2.9 fusion.109
  876.3 2.0 convert_reduce_fusion.3
  878.5 2.9 fusion.112
  881.4 79.0 %collective-permute-done.33 = f32[512,2048]{1,0:T(8,128)} collective-permute-done((f32[512,2048]{1,0:T(8,128)}, f32[512,2048]{1,0:T(8,128)}, u32[]{:S(2)}, u32[]{:S(2)}) %collective-permute-start.33) | collective-permute-done | bytes 4194336 | tf_op jit(solution)/shard_map/ppermute | solution.py:63
  960.4 2.6 collective-permute-start.28
  963.0 3.3 convolution_add_fusion.4
  966.3 17.2 %collective-permute-start.21 = (f32[1536]{0:T(1024)S(1)}, f32[1536]{0:T(1024)S(1)}, u32[]{:S(2)}, u32[]{:S(2)}) collective-permute-start(f32[1536]{0:T(1024)S(1)} %reduce_sum.188), channel_id=1, source_target_pairs={{0,1},{1,0},{2,3},{3,2},{4,5},{5,4},{6,7},{7,6},{8,9},{9,8},{10,11... | collective-permute-start | bytes 18440 | tf_op jit(solution)/shard_map/ppermute | solution.py:63
  983.4 45.1 %collective-permute-done.27 = f32[2,512]{1,0:T(2,128)S(1)} collective-permute-done((f32[2,512]{1,0:T(2,128)S(1)}, f32[2,512]{1,0:T(2,128)S(1)}, u32[]{:S(2)}, u32[]{:S(2)}) %collective-permute-start.27) | collective-permute-done | bytes 4128 | tf_op jit(solution)/shard_map/ppermute | solution.py:66
  1030.4 3.0 fusion.107
  1033.5 6.0 add_convert_fusion.2
  1040.3 24.3 %collective-permute-done.22 = f32[1536]{0:T(1024)S(1)} collective-permute-done((f32[1536]{0:T(1024)S(1)}, f32[1536]{0:T(1024)S(1)}, u32[]{:S(2)}, u32[]{:S(2)}) %collective-permute-start.22) | collective-permute-done | bytes 6176 | tf_op jit(solution)/shard_map/ppermute | solution.py:63
  1065.3 3.4 fusion.88
  1068.7 5.7 fusion.60
  1074.5 2.3 fusion.81
  1076.8 2.4 collective-permute-start.15
  1081.0 2.8 fusion.89
  1084.7 2.8 convert_reduce_fusion.6
  1093.7 3.0 copy.66
  (293 shorter events, 153.7 us)
Async XLA Ops:
  7.2 69.1 %all-gather.14.cloned.1.call-start = ((), (), s32[]{:S(2)}) async-start(), calls=%async_computation.9 | async-start | bytes 3932160 | tf_op jit(solution)/shard_map/all_gather | solution.py:112
  7.9 264.5 %all-gather.10.cloned.1.call-start = ((), (), s32[]{:S(2)}) async-start(), calls=%async_computation.4 | async-start | bytes 2621440 | tf_op jit(solution)/shard_map/all_gather | solution.py:123
  8.0 37.5 %collective-permute-start.1 = (bf16[512,1536]{1,0:T(8,128)(2,1)}, bf16[512,1536]{1,0:T(8,128)(2,1)S(1)}, u32[]{:S(2)}, u32[]{:S(2)}) collective-permute-start(bf16[512,1536]{1,0:T(8,128)(2,1)} %param.21), channel_id=1, source_target_pairs={{0,2},{1,3},{2,0},{3,1},{4,6},{5,7},{6,4},{7,5},{8,10},{9,11},{10,... | collective-permute-start | bytes 4718600 | tf_op jit(solution)/shard_map/ppermute | solution.py:63
  11.1 54.5 %collective-permute-start = (bf16[512,1536]{1,0:T(8,128)(2,1)}, bf16[512,1536]{1,0:T(8,128)(2,1)}, u32[]{:S(2)}, u32[]{:S(2)}) collective-permute-start(bf16[512,1536]{1,0:T(8,128)(2,1)} %param.21), channel_id=1, source_target_pairs={{0,1},{1,0},{2,3},{3,2},{4,5},{5,4},{6,7},{7,6},{8,9},{9,8},{10,11... | collective-permute-start | bytes 4718600 | tf_op jit(solution)/shard_map/ppermute | solution.py:63
  45.4 24.0 %collective-permute-start.2 = (bf16[512,1536]{1,0:T(8,128)(2,1)S(1)}, bf16[512,1536]{1,0:T(8,128)(2,1)S(1)}, u32[]{:S(2)}, u32[]{:S(2)}) collective-permute-start(bf16[512,1536]{1,0:T(8,128)(2,1)S(1)} %collective-permute-done.1), channel_id=1, source_target_pairs={{0,1},{1,0},{2,3},{3,2},{4,5},{5,4},{6,7},{7,6},{8,9},{9,8},{10,11... | collective-permute-start | bytes 4718600 | tf_op jit(solution)/shard_map/ppermute | solution.py:63
  45.5 310.9 %all-gather.8.cloned.1.call-start = ((), (), s32[]{:S(2)}) async-start(), calls=%async_computation.3 | async-start | bytes 3932160 | tf_op jit(solution)/shard_map/all_gather | solution.py:121
  61.1 3.1 copy-start.18
  76.3 2.8 copy-start.2
  94.6 4.0 copy-start.19
  126.7 257.9 %all-gather.16.cloned.1.call-start = ((), (), s32[]{:S(2)}) async-start(), calls=%async_computation.10 | async-start | bytes 3932160 | tf_op jit(solution)/shard_map/all_gather | solution.py:126
  126.7 17.2 %collective-permute-start.9 = (bf16[2048,512]{1,0:T(8,128)(2,1)}, bf16[2048,512]{1,0:T(8,128)(2,1)}, u32[]{:S(2)}, u32[]{:S(2)}) collective-permute-start(bf16[2048,512]{1,0:T(8,128)(2,1)} %param.29), channel_id=1, source_target_pairs={{0,0},{1,4},{2,8},{3,12},{4,1},{5,5},{6,9},{7,13},{8,2},{9,6},{10,... | collective-permute-start | bytes 6291464 | tf_op jit(solution)/shard_map/ppermute | solution.py:70
  143.9 128.5 %collective-permute-start.7 = (bf16[512,2048]{1,0:T(8,128)(2,1)}, bf16[512,2048]{1,0:T(8,128)(2,1)}, u32[]{:S(2)}, u32[]{:S(2)}) collective-permute-start(bf16[512,2048]{1,0:T(8,128)(2,1)} %param.27), channel_id=1, source_target_pairs={{0,2},{1,3},{2,0},{3,1},{4,6},{5,7},{6,4},{7,5},{8,10},{9,11},{10,... | collective-permute-start | bytes 6291464 | tf_op jit(solution)/shard_map/ppermute | solution.py:63
  143.9 129.3 %collective-permute-start.6 = (bf16[512,2048]{1,0:T(8,128)(2,1)}, bf16[512,2048]{1,0:T(8,128)(2,1)}, u32[]{:S(2)}, u32[]{:S(2)}) collective-permute-start(bf16[512,2048]{1,0:T(8,128)(2,1)} %param.27), channel_id=1, source_target_pairs={{0,1},{1,0},{2,3},{3,2},{4,5},{5,4},{6,7},{7,6},{8,9},{9,8},{10,11... | collective-permute-start | bytes 6291464 | tf_op jit(solution)/shard_map/ppermute | solution.py:63
  143.9 159.1 %collective-permute-start.11 = (bf16[2048,512]{1,0:T(8,128)(2,1)}, bf16[2048,512]{1,0:T(8,128)(2,1)}, u32[]{:S(2)}, u32[]{:S(2)}) collective-permute-start(bf16[2048,512]{1,0:T(8,128)(2,1)} %collective-permute-done.9), channel_id=1, source_target_pairs={{0,2},{1,3},{2,0},{3,1},{4,6},{5,7},{6,4},{7,5},{8,10},{9,11},{10,... | collective-permute-start | bytes 6291464 | tf_op jit(solution)/shard_map/ppermute | solution.py:63
  272.4 53.1 %collective-permute-start.4 = (bf16[512,2048]{1,0:T(8,128)(2,1)}, bf16[512,2048]{1,0:T(8,128)(2,1)}, u32[]{:S(2)}, u32[]{:S(2)}) collective-permute-start(bf16[512,2048]{1,0:T(8,128)(2,1)} %all-gather.10.cloned.1.call-done), channel_id=1, source_target_pairs={{0,2},{1,3},{2,0},{3,1},{4,6},{5,7},{6,4},{7,5},{8,10},{9,11},{10,... | collective-permute-start | bytes 6291464 | tf_op jit(solution)/shard_map/ppermute | solution.py:63
  272.4 66.4 %collective-permute-start.10 = (bf16[2048,512]{1,0:T(8,128)(2,1)}, bf16[2048,512]{1,0:T(8,128)(2,1)}, u32[]{:S(2)}, u32[]{:S(2)}) collective-permute-start(bf16[2048,512]{1,0:T(8,128)(2,1)} %collective-permute-done.9), channel_id=1, source_target_pairs={{0,1},{1,0},{2,3},{3,2},{4,5},{5,4},{6,7},{7,6},{8,9},{9,8},{10,11... | collective-permute-start | bytes 6291464 | tf_op jit(solution)/shard_map/ppermute | solution.py:63
  272.4 72.7 %collective-permute-start.8 = (bf16[512,2048]{1,0:T(8,128)(2,1)}, bf16[512,2048]{1,0:T(8,128)(2,1)}, u32[]{:S(2)}, u32[]{:S(2)}) collective-permute-start(bf16[512,2048]{1,0:T(8,128)(2,1)} %collective-permute-done.7), channel_id=1, source_target_pairs={{0,1},{1,0},{2,3},{3,2},{4,5},{5,4},{6,7},{7,6},{8,9},{9,8},{10,11... | collective-permute-start | bytes 6291464 | tf_op jit(solution)/shard_map/ppermute | solution.py:63
  272.9 286.3 %reduce-scatter.4.cloned.1.call-start = ((), (), s32[]{:S(2)}) async-start(), calls=%async_computation.5 | async-start | bytes 7864320 | tf_op jit(solution)/shard_map/reduce_scatter | solution.py:139
  273.2 73.8 %collective-permute-start.3 = (bf16[512,2048]{1,0:T(8,128)(2,1)}, bf16[512,2048]{1,0:T(8,128)(2,1)S(1)}, u32[]{:S(2)}, u32[]{:S(2)}) collective-permute-start(bf16[512,2048]{1,0:T(8,128)(2,1)} %all-gather.10.cloned.1.call-done), channel_id=1, source_target_pairs={{0,1},{1,0},{2,3},{3,2},{4,5},{5,4},{6,7},{7,6},{8,9},{9,8},{10,11... | collective-permute-start | bytes 6291464 | tf_op jit(solution)/shard_map/ppermute | solution.py:63
  303.0 50.3 %collective-permute-start.12 = (bf16[2048,512]{1,0:T(8,128)(2,1)}, bf16[2048,512]{1,0:T(8,128)(2,1)S(1)}, u32[]{:S(2)}, u32[]{:S(2)}) collective-permute-start(bf16[2048,512]{1,0:T(8,128)(2,1)} %collective-permute-done.11), channel_id=1, source_target_pairs={{0,1},{1,0},{2,3},{3,2},{4,5},{5,4},{6,7},{7,6},{8,9},{9,8},{10,11... | collective-permute-start | bytes 6291464 | tf_op jit(solution)/shard_map/ppermute | solution.py:63
  325.5 29.4 %collective-permute-start.5 = (bf16[512,2048]{1,0:T(8,128)(2,1)}, bf16[512,2048]{1,0:T(8,128)(2,1)S(1)}, u32[]{:S(2)}, u32[]{:S(2)}) collective-permute-start(bf16[512,2048]{1,0:T(8,128)(2,1)} %collective-permute-done.4), channel_id=1, source_target_pairs={{0,1},{1,0},{2,3},{3,2},{4,5},{5,4},{6,7},{7,6},{8,9},{9,8},{10,11... | collective-permute-start | bytes 6291464 | tf_op jit(solution)/shard_map/ppermute | solution.py:63
  332.9 4.3 copy-start.17
  346.9 6.4 copy-start.10
  368.8 3.3 copy-start.28
  413.5 145.7 %copy-start.7 = (bf16[768,2048]{1,0:T(8,128)(2,1)S(1)}, bf16[768,2048]{1,0:T(8,128)(2,1)}, u32[]{:S(2)}) copy-start(bf16[768,2048]{1,0:T(8,128)(2,1)} %copy-done.6) | copy-start | bytes 9437188
  413.5 214.3 %all-gather.12.cloned.1.call-start = ((), (), s32[]{:S(2)}) async-start(), calls=%async_computation.6 | async-start | bytes 3932160 | tf_op jit(solution)/shard_map/all_gather | solution.py:147
  564.2 510.2 %reduce-scatter.8.cloned.1.call-start = ((), (), s32[]{:S(2)}) async-start(), calls=%async_computation.8 | async-start | bytes 7864320 | tf_op jit(solution)/shard_map/reduce_scatter | solution.py:159
  716.0 365.0 %reduce-scatter.6.cloned.1.call-start = ((), (), s32[]{:S(2)}) async-start(), calls=%async_computation.7 | async-start | bytes 7864320 | tf_op jit(solution)/shard_map/reduce_scatter | solution.py:156
  722.8 20.5 %collective-permute-start.35 = (f32[2048,512]{1,0:T(8,128)}, f32[2048,512]{1,0:T(8,128)}, u32[]{:S(2)}, u32[]{:S(2)}) collective-permute-start(f32[2048,512]{1,0:T(8,128)} %fusion.91), channel_id=1, source_target_pairs={{0,1},{1,0},{2,3},{3,2},{4,5},{5,4},{6,7},{7,6},{8,9},{9,8},{10,11... | collective-permute-start | bytes 12582920 | tf_op jit(solution)/shard_map/ppermute | solution.py:63
  735.6 3.7 copy-start.15
  735.6 3.7 copy-start.21
  738.8 17.9 %collective-permute-start.32 = (f32[512,2048]{1,0:T(8,128)S(1)}, f32[512,2048]{1,0:T(8,128)S(1)}, u32[]{:S(2)}, u32[]{:S(2)}) collective-permute-start(f32[512,2048]{1,0:T(8,128)S(1)} %fusion.102), channel_id=1, source_target_pairs={{0,1},{1,0},{2,3},{3,2},{4,5},{5,4},{6,7},{7,6},{8,9},{9,8},{10,11... | collective-permute-start | bytes 12582920 | tf_op jit(solution)/shard_map/ppermute | solution.py:63
  743.2 6.0 copy-start.5
  743.2 22.0 %collective-permute-start.34 = (f32[2048,512]{1,0:T(8,128)}, f32[2048,512]{1,0:T(8,128)S(1)}, u32[]{:S(2)}, u32[]{:S(2)}) collective-permute-start(f32[2048,512]{1,0:T(8,128)} %fusion.94), channel_id=1, source_target_pairs={{0,1},{1,0},{2,3},{3,2},{4,5},{5,4},{6,7},{7,6},{8,9},{9,8},{10,11... | collective-permute-start | bytes 12582920 | tf_op jit(solution)/shard_map/ppermute | solution.py:63
  747.6 5.7 copy-start.8
  747.6 5.7 copy-start.13
  747.6 93.5 %collective-permute-start.36 = (f32[2048,512]{1,0:T(8,128)S(1)}, f32[2048,512]{1,0:T(8,128)S(1)}, u32[]{:S(2)}, u32[]{:S(2)}) collective-permute-start(f32[2048,512]{1,0:T(8,128)S(1)} %convolution_add_fusion.2), channel_id=1, source_target_pairs={{0,2},{1,3},{2,0},{3,1},{4,6},{5,7},{6,4},{7,5},{8,10},{9,11},{10,... | collective-permute-start | bytes 12582920 | tf_op jit(solution)/shard_map/ppermute | solution.py:63
  753.0 121.4 %collective-permute-start.31 = (f32[512,2048]{1,0:T(8,128)}, f32[512,2048]{1,0:T(8,128)}, u32[]{:S(2)}, u32[]{:S(2)}) collective-permute-start(f32[512,2048]{1,0:T(8,128)} %fusion.105), channel_id=1, source_target_pairs={{0,1},{1,0},{2,3},{3,2},{4,5},{5,4},{6,7},{7,6},{8,9},{9,8},{10,11... | collective-permute-start | bytes 12582920 | tf_op jit(solution)/shard_map/ppermute | solution.py:63
  756.5 110.0 %collective-permute-start.19 = (f32[512,1536]{1,0:T(8,128)}, f32[512,1536]{1,0:T(8,128)}, u32[]{:S(2)}, u32[]{:S(2)}) collective-permute-start(f32[512,1536]{1,0:T(8,128)} %fusion.115), channel_id=1, source_target_pairs={{0,1},{1,0},{2,3},{3,2},{4,5},{5,4},{6,7},{7,6},{8,9},{9,8},{10,11... | collective-permute-start | bytes 9437192 | tf_op jit(solution)/shard_map/ppermute | solution.py:63
  760.7 199.7 %collective-permute-start.33 = (f32[512,2048]{1,0:T(8,128)}, f32[512,2048]{1,0:T(8,128)}, u32[]{:S(2)}, u32[]{:S(2)}) collective-permute-start(f32[512,2048]{1,0:T(8,128)} %convolution_add_fusion.3), channel_id=1, source_target_pairs={{0,2},{1,3},{2,0},{3,1},{4,6},{5,7},{6,4},{7,5},{8,10},{9,11},{10,... | collective-permute-start | bytes 12582920 | tf_op jit(solution)/shard_map/ppermute | solution.py:63
  846.2 120.0 %collective-permute-start.37 = (bf16[2048,512]{1,0:T(8,128)(2,1)}, bf16[2048,512]{1,0:T(8,128)(2,1)}, u32[]{:S(2)}, u32[]{:S(2)}) collective-permute-start(bf16[2048,512]{1,0:T(8,128)(2,1)} %add_convert_fusion.1), channel_id=1, source_target_pairs={{0,0},{1,4},{2,8},{3,12},{4,1},{5,5},{6,9},{7,13},{8,2},{9,6},{10,... | collective-permute-start | bytes 6291464 | tf_op jit(solution)/shard_map/ppermute | solution.py:70
  866.5 202.2 %collective-permute-start.18 = (f32[512,1536]{1,0:T(8,128)}, f32[512,1536]{1,0:T(8,128)}, u32[]{:S(2)}, u32[]{:S(2)}) collective-permute-start(f32[512,1536]{1,0:T(8,128)} %fusion.118), channel_id=1, source_target_pairs={{0,1},{1,0},{2,3},{3,2},{4,5},{5,4},{6,7},{7,6},{8,9},{9,8},{10,11... | collective-permute-start | bytes 9437192 | tf_op jit(solution)/shard_map/ppermute | solution.py:63
  871.5 197.2 %collective-permute-start.20 = (f32[512,1536]{1,0:T(8,128)}, f32[512,1536]{1,0:T(8,128)}, u32[]{:S(2)}, u32[]{:S(2)}) collective-permute-start(f32[512,1536]{1,0:T(8,128)} %convolution_add_fusion), channel_id=1, source_target_pairs={{0,2},{1,3},{2,0},{3,1},{4,6},{5,7},{6,4},{7,5},{8,10},{9,11},{10,... | collective-permute-start | bytes 9437192 | tf_op jit(solution)/shard_map/ppermute | solution.py:63
  874.4 88.6 %collective-permute-start.24 = (f32[512,512]{1,0:T(8,128)}, f32[512,512]{1,0:T(8,128)}, u32[]{:S(2)}, u32[]{:S(2)}) collective-permute-start(f32[512,512]{1,0:T(8,128)} %fusion.109), channel_id=1, source_target_pairs={{0,1},{1,0},{2,3},{3,2},{4,5},{5,4},{6,7},{7,6},{8,9},{9,8},{10,11... | collective-permute-start | bytes 3145736 | tf_op jit(solution)/shard_map/ppermute | solution.py:63
  960.4 23.0 %collective-permute-start.28 = (f32[2,512]{1,0:T(2,128)S(1)}, f32[2,512]{1,0:T(2,128)S(1)}, u32[]{:S(2)}, u32[]{:S(2)}) collective-permute-start(f32[2,512]{1,0:T(2,128)S(1)} %get-tuple-element.111), channel_id=1, source_target_pairs={{0,12},{4,0},{8,4},{12,8},{1,13},{5,1},{9,5},{13,9},{2,14},{6,2},{... | collective-permute-start | bytes 12296 | tf_op jit(solution)/shard_map/ppermute | solution.py:66
  963.0 65.5 %collective-permute-start.27 = (f32[2,512]{1,0:T(2,128)S(1)}, f32[2,512]{1,0:T(2,128)S(1)}, u32[]{:S(2)}, u32[]{:S(2)}) collective-permute-start(f32[2,512]{1,0:T(2,128)S(1)} %get-tuple-element.110), channel_id=1, source_target_pairs={{0,8},{4,12},{8,0},{12,4},{1,9},{5,13},{9,1},{13,5},{2,10},{6,14},... | collective-permute-start | bytes 12296 | tf_op jit(solution)/shard_map/ppermute | solution.py:66
  966.3 67.2 %collective-permute-start.21 = (f32[1536]{0:T(1024)S(1)}, f32[1536]{0:T(1024)S(1)}, u32[]{:S(2)}, u32[]{:S(2)}) collective-permute-start(f32[1536]{0:T(1024)S(1)} %reduce_sum.188), channel_id=1, source_target_pairs={{0,1},{1,0},{2,3},{3,2},{4,5},{5,4},{6,7},{7,6},{8,9},{9,8},{10,11... | collective-permute-start | bytes 18440 | tf_op jit(solution)/shard_map/ppermute | solution.py:63
  983.4 81.8 %collective-permute-start.23 = (f32[512,512]{1,0:T(8,128)}, f32[512,512]{1,0:T(8,128)}, u32[]{:S(2)}, u32[]{:S(2)}) collective-permute-start(f32[512,512]{1,0:T(8,128)} %fusion.112), channel_id=1, source_target_pairs={{0,1},{1,0},{2,3},{3,2},{4,5},{5,4},{6,7},{7,6},{8,9},{9,8},{10,11... | collective-permute-start | bytes 3145736 | tf_op jit(solution)/shard_map/ppermute | solution.py:63
  1028.5 36.8 %collective-permute-start.25 = (f32[512,512]{1,0:T(8,128)}, f32[512,512]{1,0:T(8,128)}, u32[]{:S(2)}, u32[]{:S(2)}) collective-permute-start(f32[512,512]{1,0:T(8,128)} %convolution_add_fusion.4), channel_id=1, source_target_pairs={{0,2},{1,3},{2,0},{3,1},{4,6},{5,7},{6,4},{7,5},{8,10},{9,11},{10,... | collective-permute-start | bytes 3145736 | tf_op jit(solution)/shard_map/ppermute | solution.py:63
  1033.4 6.1 collective-permute-start.26
  1039.5 29.2 %copy-start.9 = (bf16[8,3,768,64]{2,3,1,0:T(8,128)(2,1)S(1)}, bf16[8,3,768,64]{2,3,1,0:T(8,128)(2,1)}, u32[]{:S(2)}) copy-start(bf16[8,3,768,64]{2,3,1,0:T(8,128)(2,1)} %get-tuple-element.56) | copy-start | bytes 7077892
  1039.5 25.1 %collective-permute-start.22 = (f32[1536]{0:T(1024)S(1)}, f32[1536]{0:T(1024)S(1)}, u32[]{:S(2)}, u32[]{:S(2)}) collective-permute-start(f32[1536]{0:T(1024)S(1)} %add.301), channel_id=1, source_target_pairs={{0,2},{1,3},{2,0},{3,1},{4,6},{5,7},{6,4},{7,5},{8,10},{9,11},{10,... | collective-permute-start | bytes 18440 | tf_op jit(solution)/shard_map/ppermute | solution.py:63
  1068.7 5.8 copy-start.11
  1068.7 5.8 copy-start.23
  1068.7 5.8 copy-start.25
  1068.7 5.8 copy-start.26
  1074.4 6.5 copy-start.27
  1076.8 7.5 collective-permute-start.15
  1079.2 5.1 collective-permute-start.14
  1079.2 5.4 collective-permute-start.13
  1080.9 2.9 collective-permute-start.16
  1083.7 3.8 collective-permute-start.17
  1087.5 1.2 collective-permute-start.29
  1088.7 3.7 collective-permute-start.30
  (11 other events, 18.0 us)
Sparse Core Ops, SparseCore 0:
  9.6 66.6 all-gather.13
  77.8 44.0 all-gather.9
  126.8 125.0 all-gather.7
  273.0 61.8 all-gather.15
  413.7 145.4 reduce-scatter.3
  564.4 63.4 all-gather.11
  716.1 109.3 reduce-scatter.7
  827.8 174.5 reduce-scatter.5

commit v2 on v1

v2 whole, which is shorter than its diff:
```python
import functools

import jax
import jax.numpy as jnp
from jax import lax
from jax.experimental import pallas as pl
from jax.experimental.pallas import tpu as pltpu
from jax.sharding import PartitionSpec as P


LN_EPS = 1e-5
BF16 = jnp.bfloat16
F32 = jnp.float32
LOG2E = 1.4426950408889634
MASKED = -1e30


def gelu_tanh(pre_act):
    return jax.nn.gelu(pre_act, approximate=True)


def dot_nn(lhs, rhs):
    return jnp.dot(lhs, rhs, preferred_element_type=F32)


def dot_nt(lhs, rhs):
    return lax.dot_general(lhs, rhs, (((1,), (1,)), ((), ())), preferred_element_type=F32)


def dot_tn(lhs, rhs):
    return lax.dot_general(lhs, rhs, (((0,), (0,)), ((), ())), preferred_element_type=F32)


def split_heads(blk, base, size):
    return blk[:, base:base + size], blk[:, base + size:base + 2 * size], blk[:, base + 2 * size:base + 3 * size]


def causal_mask(step):
    key_pos = lax.broadcasted_iota(jnp.int32, (step, step), 0)
    return key_pos <= lax.broadcasted_iota(jnp.int32, (step, step), 1)


def attn_fwd_kernel(head_dim, step, qkv_ref, out_ref, stat_ref):
    blocks = qkv_ref.shape[0] // step
    factor = head_dim ** -0.5 * LOG2E
    mask = causal_mask(step)
    blk = qkv_ref[...]
    for i in range(blocks):
        rows = slice(i * step, (i + 1) * step)
        outs = []
        for j in range(2):
            query, key, value = split_heads(blk, j * 3 * head_dim, head_dim)
            scores = [dot_nt(key[b * step:(b + 1) * step], query[rows]) for b in range(i + 1)]
            scores[i] = jnp.where(mask, scores[i], MASKED)
            top = functools.reduce(jnp.maximum, [jnp.max(s, axis=0, keepdims=True) for s in scores])
            exps = [jnp.exp2((s - top) * factor) for s in scores]
            inv = 1.0 / sum(jnp.sum(e, axis=0, keepdims=True) for e in exps)
            outs.append(sum(dot_tn(value[b * step:(b + 1) * step], (e * inv).astype(BF16)) for b, e in enumerate(exps)))
            stat_ref[0, 2 * j:2 * j + 1, rows] = top
            stat_ref[0, 2 * j + 1:2 * j + 2, rows] = inv
        out_ref[rows, :] = jnp.concatenate(outs, axis=0).T.astype(BF16)


def attn_bwd_kernel(head_dim, step, qkv_ref, grad_ref, stat_ref, out_ref):
    blocks = qkv_ref.shape[0] // step
    scale = head_dim ** -0.5
    factor = scale * LOG2E
    mask = causal_mask(step)
    blk = qkv_ref[...]
    for j in range(2):
        base = j * 3 * head_dim
        query, key, value = split_heads(blk, base, head_dim)
        grad = grad_ref[:, j * head_dim:(j + 1) * head_dim]
        grad_key, grad_value = [0.0] * blocks, [0.0] * blocks
        for i in range(blocks):
            rows = slice(i * step, (i + 1) * step)
            top = stat_ref[0, 2 * j:2 * j + 1, rows]
            inv = stat_ref[0, 2 * j + 1:2 * j + 2, rows]
            probs, grads, dots = [], [], 0.0
            for b in range(i + 1):
                keys = slice(b * step, (b + 1) * step)
                scores = dot_nt(key[keys], query[rows])
                if b == i:
                    scores = jnp.where(mask, scores, MASKED)
                prob = jnp.exp2((scores - top) * factor) * inv
                grad_prob = dot_nt(value[keys], grad[rows])
                dots = dots + jnp.sum(prob * grad_prob, axis=0, keepdims=True)
                probs.append(prob)
                grads.append(grad_prob)
            grad_query = 0.0
            for b in range(i + 1):
                keys = slice(b * step, (b + 1) * step)
                grad_score = (probs[b] * (grads[b] - dots)).astype(BF16)
                grad_value[b] = grad_value[b] + dot_nn(probs[b].astype(BF16), grad[rows])
                grad_key[b] = grad_key[b] + dot_nn(grad_score, query[rows])
                grad_query = grad_query + dot_tn(key[keys], grad_score)
            out_ref[rows, base:base + head_dim] = (grad_query.T * scale).astype(BF16)
        for b in range(blocks):
            rows = slice(b * step, (b + 1) * step)
            out_ref[rows, base + head_dim:base + 2 * head_dim] = (grad_key[b] * scale).astype(BF16)
            out_ref[rows, base + 2 * head_dim:base + 3 * head_dim] = grad_value[b].astype(BF16)


def attn_cost(tokens, heads, head_dim, dots):
    return pl.CostEstimate(flops=dots * tokens * tokens * heads * head_dim, bytes_accessed=12 * tokens * heads * head_dim, transcendentals=tokens * tokens * heads // 2)


def attn_forward(qkv_rows, head_dim):
    tokens, width = qkv_rows.shape
    pairs = width // (6 * head_dim)
    return pl.pallas_call(
        functools.partial(attn_fwd_kernel, head_dim, 256),
        grid=(pairs,),
        in_specs=[pl.BlockSpec((tokens, 6 * head_dim), lambda p: (0, p))],
        out_specs=[pl.BlockSpec((tokens, 2 * head_dim), lambda p: (0, p)), pl.BlockSpec((1, 8, tokens), lambda p: (p, 0, 0))],
        out_shape=[jax.ShapeDtypeStruct((tokens, 2 * head_dim * pairs), BF16), jax.ShapeDtypeStruct((pairs, 8, tokens), F32)],
        cost_estimate=attn_cost(tokens, 2 * pairs, head_dim, 4),
        name="attn_fwd",
    )(qkv_rows)


def attn_backward(qkv_rows, grad_rows, stats, head_dim):
    tokens, width = qkv_rows.shape
    pairs = width // (6 * head_dim)
    return pl.pallas_call(
        functools.partial(attn_bwd_kernel, head_dim, 256),
        grid=(pairs,),
        in_specs=[pl.BlockSpec((tokens, 6 * head_dim), lambda p: (0, p)), pl.BlockSpec((tokens, 2 * head_dim), lambda p: (0, p)), pl.BlockSpec((1, 8, tokens), lambda p: (p, 0, 0))],
        out_specs=pl.BlockSpec((tokens, 6 * head_dim), lambda p: (0, p)),
        out_shape=jax.ShapeDtypeStruct((tokens, width), BF16),
        cost_estimate=attn_cost(tokens, 2 * pairs, head_dim, 10),
        name="attn_bwd",
    )(qkv_rows, grad_rows, stats)


def place_kernel(count, index_ref, *refs):
    for part in range(count):
        @pl.when(pl.program_id(0) == part)
        def _():
            refs[count][...] = refs[part][0]


def place_blocks(parts, where, shape, tile):
    count = len(parts)
    depth, rows, cols = parts[0].shape
    steps = rows // tile

    def part_map(own):
        def index_map(part, level, step, index_ref):
            active, past = part == own, part > own
            last = jnp.where(past, 1, 0)
            return jnp.where(active, level, last * (depth - 1)), jnp.where(active, step, last * (steps - 1)), 0

        return index_map

    def out_map(part, level, step, index_ref):
        slot = 2 * (part * depth + level)
        return index_ref[slot] * steps + step, index_ref[slot + 1]

    return pl.pallas_call(
        functools.partial(place_kernel, count),
        grid_spec=pltpu.PrefetchScalarGridSpec(
            num_scalar_prefetch=1,
            grid=(count, depth, steps),
            in_specs=[pl.BlockSpec((1, tile, cols), part_map(own)) for own in range(count)],
            out_specs=pl.BlockSpec((tile, cols), out_map),
        ),
        out_shape=jax.ShapeDtypeStruct(shape, parts[0].dtype),
        cost_estimate=pl.CostEstimate(flops=40000000, bytes_accessed=4 * shape[0] * shape[1], transcendentals=0),
        name="place_blocks",
    )(jnp.stack(where).astype(jnp.int32), *parts)


def norm_stats(act_f32, width):
    mean_val = jnp.sum(act_f32, axis=-1, keepdims=True) / width
    mean_sq = jnp.sum(act_f32 * act_f32, axis=-1, keepdims=True) / width
    return mean_val, lax.rsqrt(mean_sq - mean_val * mean_val + LN_EPS)


def solution(mesh):
    n_row, n_col = mesh.shape['row'], mesh.shape['col']
    act_spec = P(('dp', 'row'), None, 'col')
    vec_spec = P('col')
    mat_spec = P('row', 'col')
    head_spec = P('col', None)
    gvec_spec = P(('dp', 'col'))
    gmat_spec = P(('dp', 'row'), 'col')
    ghead_spec = P(('dp', 'col'), None)

    def flip_row(val, bits):
        return lax.ppermute(val, 'row', [(src, src ^ bits) for src in range(n_row)])

    def shift_col(val, step):
        return lax.ppermute(val, 'col', [(src, (src + step) % n_col) for src in range(n_col)])

    def cross(val, route):
        pairs = []
        for r in range(n_row):
            for c in range(n_col):
                row_to, col_to = route(r, c)
                if (row_to, col_to) != (r, c):
                    pairs.append((c * n_row + r, col_to * n_row + row_to))
        return lax.ppermute(val, ('col', 'row'), pairs)

    def cross_even(val):
        moved = cross(val, lambda r, c: (c, r))
        return jnp.where(lax.axis_index('row') == lax.axis_index('col'), val, moved)

    def pick(first, lead, other):
        return jnp.where(first, lead, other), jnp.where(first, other, lead)

    def tie(val, *others):
        return lax.optimization_barrier((val,) + others)[0]

    def swap_dp(val):
        return lax.ppermute(val, 'dp', [(0, 1), (1, 0)])

    def join_dp(half, axis):
        other = swap_dp(half)
        lead = lax.axis_index('dp') == 0
        return jnp.concatenate([jnp.where(lead, half, other), jnp.where(lead, other, half)], axis=axis)

    def half_dp(val, axis):
        size = val.shape[axis] // 2
        return lax.dynamic_slice_in_dim(val, lax.axis_index('dp') * size, size, axis)

    def gather_row(w_blk, far):
        row = lax.axis_index('row')
        mate = flip_row(w_blk, 1)
        far_mate = flip_row(far, 1)
        parts = [part[None] for part in (w_blk, mate, far, far_mate)]
        where = [coord for bits in range(4) for coord in (row ^ bits, jnp.zeros_like(row))]
        return place_blocks(parts, where, (n_row * w_blk.shape[0], w_blk.shape[1]), w_blk.shape[0])

    def scatter_near(make_part):
        row = lax.axis_index('row')
        got_far = flip_row(make_part(row ^ 3), 1)
        got_own = flip_row(make_part(row ^ 1), 1)
        return make_part(row ^ 2) + got_far, got_own

    def scatter_far(make_part, got_own, far):
        return (make_part(lax.axis_index('row')) + got_own + far).astype(BF16)

    def sum_row(val):
        val = val + flip_row(val, 1)
        return val + flip_row(val, 2)

    def layer_block(x_blk, ln1_scale, ln1_shift, w_qkv, b_qkv, w_o, b_o, ln2_scale, ln2_shift, w_in, b_in, w_out, b_out, grad_blk):
        seq_count, seq_len, d_local = x_blk.shape
        tokens = seq_count * seq_len
        heads_local, qkv_width = b_qkv.shape
        head_dim = qkv_width // 3
        width = d_local * n_col
        col = lax.axis_index('col')
        x_rows = x_blk.reshape(tokens, d_local)
        grad_rows = grad_blk.reshape(tokens, d_local)

        def col_block(val, axis, index, size):
            return lax.dynamic_slice_in_dim(val, index * size, size, axis)

        row = lax.axis_index('row')
        near_y = row // 2

        def spread(tok_vals):
            full = jnp.zeros((tokens, d_local), tok_vals.dtype)
            size = tokens // n_col
            for step in range(n_col):
                part = col_block(tok_vals, 1, (col + step) % n_col, d_local)
                part = shift_col(part, step) if step else part
                full = lax.dynamic_update_slice_in_dim(full, part, (col - step) % n_col * size, 0)
            return full

        vec_blk = jnp.stack([ln1_scale, ln1_shift, b_o, ln2_scale, ln2_shift])
        vec_far = [shift_col(vec_blk, step) for step in range(1, n_col)]
        vecs = jnp.zeros((5, width), F32)
        for step, part in enumerate([vec_blk] + vec_far):
            vecs = lax.dynamic_update_slice_in_dim(vecs, part, (col - step) % n_col * d_local, 1)
        s1, t1, bo, s2, t2 = [vecs[i:i + 1] for i in range(5)]

        wo_half = lax.all_gather(half_dp(w_o, 0), 'col', axis=1, tiled=True)
        x_full = lax.all_gather(tie(x_rows, wo_half), 'col', axis=1, tiled=True)
        wq_far = flip_row(w_qkv, 2)
        wo_pair = join_dp(wo_half, 0)
        wi_far = flip_row(tie(w_in, wq_far), 2)
        wi = gather_row(w_in, wi_far)
        wo_far = flip_row(tie(wo_pair, wi_far), 2)
        half_f = w_out.shape[0] // 2
        wq = gather_row(w_qkv, wq_far)
        x_full = tie(x_full, *vec_far)
        w_half = tie(half_dp(w_out, 1), x_full)
        wt_even = cross_even(col_block(w_half, 0, col // 2, half_f))
        wt_odd = cross(col_block(w_half, 0, 1 - col // 2, half_f), lambda r, c: (c ^ 2, r))
        wt_half = jnp.stack(pick(near_y == 0, wt_even, wt_odd))
        x32 = x_full.astype(F32)
        mean1, inv1 = norm_stats(x32, width)
        h1 = ((x32 - mean1) * inv1 * s1 + t1).astype(BF16)
        qkv_dot = dot_nn(h1, wq)
        qkv_rows = (qkv_dot + b_qkv.reshape(heads_local * qkv_width)).astype(BF16)
        attn_rows, attn_stats = attn_forward(qkv_rows, head_dim)
        attn_full = lax.all_gather(attn_rows, 'col', axis=1, tiled=True)

        g_full = lax.all_gather(tie(grad_rows, attn_rows), 'col', axis=1, tiled=True)
        wo = gather_row(wo_pair, wo_far)
        wt_pair = join_dp(wt_half, 2)
        wt_far = flip_row(tie(wt_pair, wo_far), 2)
        attn_full = tie(attn_full, wt_pair)

        r1_dot = dot_nn(attn_full, wo)
        r1 = (x32 + r1_dot + bo).astype(BF16)
        wt_far = tie(wt_far, r1)
        wt_parts = [wt_pair, flip_row(wt_pair, 1), wt_far, flip_row(wt_far, 1)]
        where = [coord for half in (near_y, 1 - near_y) for bit in range(2) for j in range(2) for coord in (half, 2 * j + (row % 2 ^ bit))]
        wt = place_blocks(wt_parts, where, (2 * half_f, width), half_f)
        r32 = r1.astype(F32)
        mean2, inv2 = norm_stats(r32, width)
        h2 = ((r32 - mean2) * inv2 * s2 + t2).astype(BF16)
        pre_act = dot_nn(h2, wi) + b_in
        hidden, gelu_back = jax.vjp(gelu_tanh, pre_act)
        hidden = hidden.astype(BF16)

        out_dot = dot_nn(hidden, wt)
        out_part = lax.psum_scatter(out_dot, 'col', scatter_dimension=1, tiled=True)
        grad_hidden = dot_nt(tie(g_full, out_dot), wt).astype(BF16)
        grad_pre = gelu_back(grad_hidden.astype(F32))[0].astype(BF16)
        tok_local = tokens // n_col
        gn2_dot = dot_nt(grad_pre, wi)
        k_local = width // n_row
        hidden_l, g_l, h2_l, gp_l = lax.optimization_barrier((hidden, g_full, h2, grad_pre, gn2_dot))[:4]

        def wout_part(half, core):
            pair = jnp.concatenate([col_block(g_l, 1, core, d_local), col_block(g_l, 1, 2 + core, d_local)], axis=1)
            return dot_tn(col_block(hidden_l, 1, half, half_f), pair)

        make_win = lambda j: dot_tn(col_block(h2_l, 1, j, k_local), gp_l)
        core = row % 2
        wout_got = flip_row(wout_part(1 - near_y, 1 - core), 1)
        wout_own = flip_row(wout_part(near_y, 1 - core), 1)
        wout_send = wout_part(1 - near_y, core) + wout_got
        wout_far = flip_row(wout_send, 2)
        win_send, win_own = scatter_near(make_win)
        win_far = flip_row(tie(win_send, wout_far), 2)
        gn2 = lax.psum_scatter(tie(gn2_dot, out_part, wout_send, win_send), 'col', scatter_dimension=0, tiled=True)
        wout_sum = (wout_part(near_y, core) + wout_own + wout_far).astype(BF16)
        gn2 = tie(gn2, wout_sum).astype(BF16).astype(F32)
        r_tok = col_block(r1, 0, col, tok_local).astype(F32)
        mean_t, inv_t = col_block(mean2, 0, col, tok_local), col_block(inv2, 0, col, tok_local)
        hat_t = (r_tok - mean_t) * inv_t
        gs2 = jnp.stack([jnp.sum(gn2 * hat_t, axis=0), jnp.sum(gn2, axis=0)])
        ghat = gn2 * s2
        gin = inv_t * (ghat - jnp.mean(ghat, axis=-1, keepdims=True) - hat_t * jnp.mean(ghat * hat_t, axis=-1, keepdims=True))
        gr_tok = (col_block(g_full, 0, col, tok_local).astype(F32) + gin).astype(BF16)
        grad_attn = spread(dot_nt(gr_tok, wo).astype(BF16))
        wout_even = cross_even(col_block(tie(wout_sum, grad_attn), 1, near_y, d_local))
        wout_odd = cross(col_block(tie(wout_sum, grad_attn), 1, 1 - near_y, d_local), lambda r, c: (c, r ^ 2))
        grad_qkv = attn_backward(qkv_rows, grad_attn, attn_stats, head_dim)
        out_rows = (col_block(r1, 1, col, d_local).astype(F32) + out_part + b_out).astype(BF16)

        grad_wout = jnp.concatenate(pick(col // 2 == 0, wout_even, wout_odd), axis=0)
        gn1_dot = dot_nt(grad_qkv, wq)
        gn1 = lax.psum_scatter(gn1_dot, 'col', scatter_dimension=1, tiled=True)
        h1_l, gq_l = lax.optimization_barrier((h1, grad_qkv, gn1_dot))[:2]
        make_wqkv = lambda j: dot_tn(col_block(h1_l, 1, j, k_local), gq_l)
        wqkv_send, wqkv_own = scatter_near(make_wqkv)
        wqkv_far = flip_row(wqkv_send, 2)
        gr_mine = spread(tie(gr_tok, wqkv_send))
        make_wo = lambda j: dot_tn(col_block(attn_full, 1, j, k_local), gr_mine)
        wo_send, wo_own = scatter_near(make_wo)
        gwo_far = flip_row(wo_send, 2)
        grad_wqkv = scatter_far(make_wqkv, wqkv_own, wqkv_far)
        grad_win = scatter_far(make_win, win_own, win_far)
        grad_wo = scatter_far(make_wo, wo_own, gwo_far)
        gn1 = tie(gn1, grad_wqkv, grad_win).astype(BF16).astype(F32)
        hat1 = (x_rows.astype(F32) - mean1) * inv1
        ghat1 = gn1 * ln1_scale
        sums = jnp.stack([jnp.sum(ghat1, axis=-1), jnp.sum(ghat1 * hat1, axis=-1)])
        sums = (sums + shift_col(sums, 1) + shift_col(sums, 2) + shift_col(sums, 3)) / width
        gx = gr_mine.astype(F32) + inv1 * (ghat1 - sums[0][:, None] - hat1 * sums[1][:, None])
        grad_x = gx.astype(BF16)

        def tok_sum(val):
            return jnp.sum(val.astype(F32), axis=0)

        ln2_part = col_block(gs2, 1, col, d_local)
        for step in range(1, n_col):
            ln2_part = ln2_part + shift_col(col_block(gs2, 1, (col + step) % n_col, d_local), step)
        early = sum_row(jnp.concatenate([ln2_part.reshape(-1), tok_sum(grad_rows), tok_sum(gr_mine), tok_sum(grad_pre)]))
        gl2s, gl2t, gbout, gbo, gbin = jnp.split(early, [d_local * k for k in range(1, 5)])
        gbqkv = sum_row(tok_sum(grad_qkv))
        late = sum_row(jnp.stack([jnp.sum(gn1 * hat1, axis=0), jnp.sum(gn1, axis=0)]))
        return (out_rows.reshape(x_blk.shape), grad_x.reshape(x_blk.shape), late[0], late[1], grad_wqkv, gbqkv.reshape(heads_local, qkv_width), grad_wo, gbo, gl2s, gl2t, grad_win, gbin, grad_wout, gbout)

    return jax.shard_map(layer_block, mesh=mesh,
                         in_specs=(act_spec, vec_spec, vec_spec, mat_spec, head_spec, mat_spec, vec_spec, vec_spec, vec_spec, mat_spec, vec_spec, mat_spec, vec_spec, act_spec),
                         out_specs=(act_spec, act_spec, gvec_spec, gvec_spec, gmat_spec, ghead_spec, gmat_spec, gvec_spec, gvec_spec, gvec_spec, gmat_spec, gvec_spec, gmat_spec, gvec_spec),
                         check_vma=False)
```

time: 1120 us -> 907 us (0.81)
  starting transfers between devices: 199 us -> 97.2 us
  matrix products: 229 us -> 158 us
  Pallas kernels: 0 us -> 60.5 us
  local copies, waits for them, and re-layouts: 72.8 us -> 20.6 us
  waiting for transfers between devices: 524 us -> 509 us
  blocking collectives: 14 us -> 0 us
    ppermute x30, starting transfers between devices: 158 us -> 33.3 us  [flip_row(): return lax.ppermute(val, 'row', [(src, src ^ bits) for src in range(n_row)])]
    dot_general x56 -> x0, matrix products: 83.4 us -> none  [the longest x32 46.6 us: attend_one(): lax.dot_general(query_rows, key_rows, (((1,), (1,)), ((), ())), preferred...]
    reduce_scatter x3, waiting for transfers between devices: 145 us -> 75 us  [the longest x1 68.3 us: layer_block(): out_part = lax.psum_scatter(out_dot, 'col', scatter_dimension=1, tiled=True)]
    pallas_call x0 -> x6, Pallas kernels: none -> 60.5 us  [the longest x4 33.3 us: place_blocks(): pl.pallas_call(functools.partial(place_kernel, count), grid_spec=pltpu.Pr...]
    ppermute x6 -> x15, starting transfers between devices: 6.72 us -> 53.6 us  [shift_col(): lax.ppermute(val, 'col', [(src, (src + step) % n_col) for src in range(n_...]
    ppermute x2 -> x6, waiting for transfers between devices: 0.01 us -> 38.6 us  [the longest x2 24 us: swap_dp(): return lax.ppermute(val, 'dp', [(0, 1), (1, 0)])]
    ppermute x6 -> x15, waiting for transfers between devices: 45.4 us -> 81.2 us  [shift_col(): lax.ppermute(val, 'col', [(src, (src + step) % n_col) for src in range(n_...]
    dynamic_update_slice x16 -> x10, local copies, waits for them, and re-layouts: 32.6 us -> 2.13 us  [the longest x6 2.12 us: spread(): lax.dynamic_update_slice_in_dim(full, part, (col - step) % n_col * size, 0)]
  transfers between devices with their start and end apart: 46 -> 58, of which waited for: 13 -> 29; matrix products, arithmetic and copies ran while one was open for 19% -> 20% of each run, Pallas kernels for 0% -> 5%
where the time goes in v2:
time: 907 us; the launch traced here: 898 us
  waiting for transfers between devices  509 us (56%)
  matrix products  158 us (17%)
  starting transfers between devices  97.2 us (11%)
  Pallas kernels  60.5 us (7%)
  other arithmetic  37.9 us (4%)
  local copies, waits for them, and re-layouts  20.6 us (2%)
  between operations  15.3 us (2%)
    ppermute x30, waiting for transfers between devices, flip_row(): return lax.ppermute(val, 'row', [(src, src ^ bits) for src in range(n_row)])  268 us
    ppermute x15, waiting for transfers between devices, shift_col(): lax.ppermute(val, 'col', [(src, (src + step) % n_col) for src in range(n_...  81.2 us
    dot_general x16, matrix products, dot_tn(): lax.dot_general(lhs, rhs, (((0,), (0,)), ((), ())), preferred_element_typ...  70.8 us
    reduce_scatter x1, waiting for transfers between devices, layer_block(): out_part = lax.psum_scatter(out_dot, 'col', scatter_dimension=1, tiled=True)  68.3 us
    ppermute x15, starting transfers between devices, shift_col(): lax.ppermute(val, 'col', [(src, (src + step) % n_col) for src in range(n_...  53.6 us
    dot_general x4, matrix products, dot_nn(): return jnp.dot(lhs, rhs, preferred_element_type=F32)  44.3 us
    dot_general x4, matrix products, dot_nt(): lax.dot_general(lhs, rhs, (((1,), (1,)), ((), ())), preferred_element_typ...  42.5 us
    pallas_call x4, Pallas kernels, place_blocks(): pl.pallas_call(functools.partial(place_kernel, count), grid_spec=pltpu.Pr...  33.3 us
  transfers between devices with their start and end apart: 58, of which 29 were waited for; matrix products, arithmetic and copies ran while one was open for 20% of the time, Pallas kernels for 5%

profile of v2, /device:TPU:0, one launch (start us, length us, event | category | flops | bytes accessed | tf_op | source)
XLA Modules:
  0.0 898.1 jit_solution(1738226400469221308)
XLA Ops:
  9.1 31.8 %all-gather.5.cloned.1.call-done = bf16[256,2048]{1,0:T(8,128)(2,1)} async-done(((bf16[256,512]{1,0:T(8,128)(2,1)}), bf16[256,2048]{1,0:T(8,128)(2,1)}) %all-gather.5.cloned.1.call-update) | async-done | bytes 1048592 | tf_op jit(solution)/shard_map/all_gather | solution.py:280
  44.0 33.0 %collective-permute-done.4 = bf16[512,1536]{1,0:T(8,128)(2,1)} collective-permute-done((bf16[512,1536]{1,0:T(8,128)(2,1)}, bf16[512,1536]{1,0:T(8,128)(2,1)}, u32[]{:S(2)}, u32[]{:S(2)}) %collective-permute-start.4) | collective-permute-done | bytes 1572896 | tf_op jit(solution)/shard_map/ppermute | solution.py:191
  85.4 4.6 collective-permute-done.2
  91.6 2.7 broadcast_select_fusion.4
  94.2 6.6 place_blocks.4
  100.8 5.8 all-gather.7.cloned.1.call-done
  106.6 3.0 convert_reduce_fusion
  109.7 2.8 fusion.18
  113.6 8.2 add_convert_fusion.qkv_ref
  121.8 12.0 %attn_fwd.1 = (bf16[768,512]{1,0:T(8,128)(2,1)}, f32[4,8,768]{2,1,0:T(8,128)}) custom-call(bf16[768,1536]{1,0:T(8,128)(2,1)} %add_convert_fusion.qkv_ref), custom_call_target="tpu_custom_call" | custom-call | flops 1207959552 | bytes 4718592 | tf_op jit(solution)/shard_map/attn_fwd/pallas_call | solution.py:111
  133.9 3.8 pad_maximum_fusion.1
  143.3 52.1 %collective-permute-done.12 = bf16[512,2048]{1,0:T(8,128)(2,1)} collective-permute-done((bf16[512,2048]{1,0:T(8,128)(2,1)}, bf16[512,2048]{1,0:T(8,128)(2,1)}, u32[]{:S(2)}, u32[]{:S(2)}) %collective-permute-start.12) | collective-permute-done | bytes 2097184 | tf_op jit(solution)/shard_map/ppermute | solution.py:191
  195.4 14.6 %collective-permute-done.7 = bf16[1024,256]{1,0:T(8,128)(2,1)S(1)} collective-permute-done((bf16[1024,256]{1,0:T(8,128)(2,1)}, bf16[1024,256]{1,0:T(8,128)(2,1)S(1)}, u32[]{:S(2)}, u32[]{:S(2)}) %collective-permute-start.7) | collective-permute-done | bytes 524320 | tf_op jit(solution)/shard_map/ppermute | solution.py:203
  211.8 24.0 %collective-permute-done.8 = bf16[2,1024,256]{2,1,0:T(8,128)(2,1)S(1)} collective-permute-done((bf16[2,1024,256]{2,1,0:T(8,128)(2,1)S(1)}, bf16[2,1024,256]{2,1,0:T(8,128)(2,1)S(1)}, u32[]{:S(2)}, u32[]{:S(2)}) %collective-permute-start.8) | collective-permute-done | bytes 1048608 | tf_op jit(solution)/shard_map/ppermute | solution.py:216
  237.5 16.3 %collective-permute-start.17 = (bf16[2,1024,512]{2,1,0:T(8,128)(2,1)}, bf16[2,1024,512]{2,1,0:T(8,128)(2,1)}, u32[]{:S(2)}, u32[]{:S(2)}) collective-permute-start(bf16[2,1024,512]{2,1,0:T(8,128)(2,1)} %pad_maximum_fusion.refs_0_), channel_id=1, source_target_pairs={{0,2},{1,3},{2,0},{3,1},{4,6},{5,7},{6,4},{7,5},{8,10},{9,11},{10,... | collective-permute-start | bytes 6291464 | tf_op jit(solution)/shard_map/ppermute | solution.py:191
  255.7 7.8 place_blocks.6
  263.9 8.1 place_blocks.5
  271.9 10.6 %convert_reduce_fusion.1 = (f32[768]{0:T(1024)S(1)}, f32[768]{0:T(1024)S(1)}, bf16[768,2048]{1,0:T(8,128)(2,1)S(1)}) fusion(f32[2048]{0:T(1024)S(1)} %bitcast.107, bf16[768,2048]{1,0:T(8,128)(2,1)} %all-gather.9.cloned.1.call-done, bf16[2048,2048]{1,0:T(8,128)(2,1)} %place_blocks.5, bf16[768,2048]{1,0:T(8,128)(2,1)S(1)} %copy-done.8), kind=kOutput, calls=%fused_computation.6 | convolution fusion | flops 6455031808 | bytes 17840128 | tf_op jit(solution)/shard_map/dot_general | solution.py:23
  282.6 3.5 collective-permute-done.17.refs_2_
  287.4 13.7 %multiply_convert_fusion = (bf16[768,2048]{1,0:T(8,128)(2,1)}, f32[768,2048]{1,0:T(8,128)}) fusion(f32[2048]{0:T(1024)S(1)} %copy-done.30, bf16[768,2048]{1,0:T(8,128)(2,1)S(1)} %fusion.13, bf16[2048,2048]{1,0:T(8,128)(2,1)} %place_blocks.6), kind=kOutput, calls=%fused_computation.34 | convolution fusion | flops 6458179584 | bytes 20979712 | tf_op jit(solution)/shard_map/dot_general | solution.py:23
  302.4 10.9 %place_blocks.7 = bf16[2048,2048]{1,0:T(8,128)(2,1)} custom-call(s32[16]{0:T(128)} %stack.130.index_ref, bf16[2,1024,512]{2,1,0:T(8,128)(2,1)} %pad_maximum_fusion.refs_0_, bf16[2,1024,512]{2,1,0:T(8,128)(2,1)} %collective-permute-done.16.refs_1_, bf16[2,1024,512]{2,1,0:T(8,128)(2,1)} %collective-permute-done.17.refs_2_, bf16[2,1024,512]{2,1,0:T(8,128)(2,1)} %copy-done.16), custom_call_target="tpu_custom_call" | custom-call | flops 40000000 | bytes 16777216 | tf_op jit(solution)/shard_map/place_blocks/pallas_call | solution.py:160
  313.3 11.8 %fusion.100 = f32[768,2048]{1,0:T(8,128)} fusion(bf16[768,2048]{1,0:T(8,128)(2,1)} %get-tuple-element.49, bf16[2048,2048]{1,0:T(8,128)(2,1)} %place_blocks.7), kind=kOutput, calls=%fused_computation.202 | convolution fusion | flops 6442450944 | bytes 17825792 | tf_op jit(solution)/shard_map/dot_general | solution.py:23
  325.5 8.5 all-gather.11.cloned.1.call-done
  334.0 15.3 %convert_reduce_fusion.2 = (f32[2048]{0:T(1024)}, bf16[768,2048]{1,0:T(8,128)(2,1)S(1)}) fusion(f32[768,2048]{1,0:T(8,128)} %get-tuple-element.126, f32[2048]{0:T(1024)S(1)} %copy-done.30, bf16[768,2048]{1,0:T(8,128)(2,1)} %all-gather.11.cloned.1.call-done, bf16[2048,2048]{1,0:T(8,128)(2,1)} %place_blocks.7), kind=kOutput, calls=%fused_computation.33 | convolution fusion | flops 6481770496 | bytes 20987904 | tf_op jit(solution)/shard_map/dot_general | solution.py:27
  349.2 11.2 %fusion.101 = f32[768,2048]{1,0:T(8,128)} fusion(bf16[768,2048]{1,0:T(8,128)(2,1)S(1)} %get-tuple-element.52, bf16[2048,2048]{1,0:T(8,128)(2,1)} %place_blocks.6), kind=kOutput, calls=%fused_computation.203 | convolution fusion | flops 6442450944 | bytes 17825792 | tf_op jit(solution)/shard_map/dot_general | solution.py:27
  360.4 3.4 constant_dynamic-slice_fusion.10
  363.8 3.8 fusion.44
  367.6 5.0 fusion.67
  375.1 6.9 convolution_add_fusion.3
  382.0 6.3 convolution_add_fusion.2
  388.4 68.3 %reduce-scatter.4.cloned.1.call-done = f32[768,512]{1,0:T(8,128)} async-done(((f32[768,2048]{1,0:T(8,128)}), f32[768,512]{1,0:T(8,128)}) %reduce-scatter.4.cloned.1.call-update) | async-done | bytes 1572880 | tf_op jit(solution)/shard_map/reduce_scatter | solution.py:322
  456.9 5.7 fusion.41
  464.2 5.9 collective-permute-done.21
  470.1 85.8 %collective-permute-done.22 = f32[1024,1024]{1,0:T(8,128)} collective-permute-done((f32[1024,1024]{1,0:T(8,128)}, f32[1024,1024]{1,0:T(8,128)}, u32[]{:S(2)}, u32[]{:S(2)}) %collective-permute-start.22) | collective-permute-done | bytes 4194336 | tf_op jit(solution)/shard_map/ppermute | solution.py:191
  555.9 7.5 add_convert_fusion.2
  563.4 6.7 reduce-scatter.6.cloned.1.call-done
  570.1 2.5 fusion.39
  574.7 6.6 convolution_convert_fusion.1
  586.3 2.9 collective-permute-start.25
  589.2 3.9 collective-permute-done.23
  593.7 6.5 collective-permute-done.24
  601.7 15.1 %attn_bwd.1 = bf16[768,1536]{1,0:T(8,128)(2,1)} custom-call(bf16[768,1536]{1,0:T(8,128)(2,1)} %add_convert_fusion.qkv_ref, bf16[768,512]{1,0:T(8,128)(2,1)} %constant_dynamic-update-slice_fusion.3.grad_ref, f32[4,8,768]{2,1,0:T(8,128)} %get-tuple-element.55.stat_ref), custom_call_target="tpu_custom_call" | custom-call | flops 3019898880 | bytes 4718592 | tf_op jit(solution)/shard_map/attn_bwd/pallas_call | solution.py:125
  616.8 9.5 %fusion.102 = f32[768,2048]{1,0:T(8,128)} fusion(bf16[768,1536]{1,0:T(8,128)(2,1)} %attn_bwd.1, bf16[2048,1536]{1,0:T(8,128)(2,1)} %place_blocks.4), kind=kOutput, calls=%fused_computation.204 | convolution fusion | flops 4831838208 | bytes 14942208 | tf_op jit(solution)/shard_map/dot_general | solution.py:27
  626.4 5.0 fusion.64
  631.4 5.0 fusion.57
  639.7 6.2 collective-permute-start.46
  645.9 5.0 fusion.61
  650.9 5.3 convolution_add_fusion.1
  657.5 12.7 %collective-permute-done.27 = bf16[192,512]{1,0:T(8,128)(2,1)S(1)} collective-permute-done((bf16[192,512]{1,0:T(8,128)(2,1)S(1)}, bf16[192,512]{1,0:T(8,128)(2,1)S(1)}, u32[]{:S(2)}, u32[]{:S(2)}) %collective-permute-start.27) | collective-permute-done | bytes 196640 | tf_op jit(solution)/shard_map/ppermute | solution.py:194
  672.4 10.2 %collective-permute-done.28 = bf16[192,512]{1,0:T(8,128)(2,1)S(1)} collective-permute-done((bf16[192,512]{1,0:T(8,128)(2,1)S(1)}, bf16[192,512]{1,0:T(8,128)(2,1)S(1)}, u32[]{:S(2)}, u32[]{:S(2)}) %collective-permute-start.28) | collective-permute-done | bytes 196640 | tf_op jit(solution)/shard_map/ppermute | solution.py:194
  682.6 4.0 collective-permute-done.29
  689.1 40.7 %collective-permute-done.33 = f32[512,2048]{1,0:T(8,128)} collective-permute-done((f32[512,2048]{1,0:T(8,128)}, f32[512,2048]{1,0:T(8,128)}, u32[]{:S(2)}, u32[]{:S(2)}) %collective-permute-start.33) | collective-permute-done | bytes 4194336 | tf_op jit(solution)/shard_map/ppermute | solution.py:191
  729.8 3.7 collective-permute-start.50
  733.5 3.0 fusion.59
  740.4 31.7 %collective-permute-done.45 = f32[2,512]{1,0:T(2,128)S(1)} collective-permute-done((f32[2,512]{1,0:T(2,128)S(1)}, f32[2,512]{1,0:T(2,128)S(1)}, u32[]{:S(2)}, u32[]{:S(2)}) %collective-permute-start.45) | collective-permute-done | bytes 4128 | tf_op jit(solution)/shard_map/ppermute | solution.py:194
  772.2 28.5 %collective-permute-start.44 = (f32[2,512]{1,0:T(2,128)S(1)}, f32[2,512]{1,0:T(2,128)S(1)}, u32[]{:S(2)}, u32[]{:S(2)}) collective-permute-start(f32[2,512]{1,0:T(2,128)S(1)} %get-tuple-element.115), channel_id=1, source_target_pairs={{0,4},{4,8},{8,12},{12,0},{1,5},{5,9},{9,13},{13,1},{2,6},{6,10},{... | collective-permute-start | bytes 12296 | tf_op jit(solution)/shard_map/ppermute | solution.py:194
  802.3 2.7 collective-permute-done.44
  805.8 5.0 collective-permute-start.40
  812.3 11.3 %collective-permute-done.40 = f32[1536]{0:T(1024)S(1)} collective-permute-done((f32[1536]{0:T(1024)S(1)}, f32[1536]{0:T(1024)S(1)}, u32[]{:S(2)}, u32[]{:S(2)}) %collective-permute-start.40) | collective-permute-done | bytes 6176 | tf_op jit(solution)/shard_map/ppermute | solution.py:191
  823.8 6.3 add_convert_fusion.1
  834.0 30.1 %collective-permute-done.43 = f32[512,512]{1,0:T(8,128)S(1)} collective-permute-done((f32[512,512]{1,0:T(8,128)}, f32[512,512]{1,0:T(8,128)S(1)}, u32[]{:S(2)}, u32[]{:S(2)}) %collective-permute-start.43) | collective-permute-done | bytes 1048608 | tf_op jit(solution)/shard_map/ppermute | solution.py:191
  864.1 2.5 fusion.48
  866.7 5.9 fusion.23
  872.6 2.6 fusion.40
  (222 shorter events, 80.7 us)
Async XLA Ops:
  7.2 132.0 %copy-start = (bf16[2048,512]{1,0:T(8,128)(2,1)S(1)}, bf16[2048,512]{1,0:T(8,128)(2,1)}, u32[]{:S(2)}) copy-start(bf16[2048,512]{1,0:T(8,128)(2,1)} %param.25) | copy-start | bytes 6291460
  7.2 33.7 %all-gather.5.cloned.1.call-start = ((), (), s32[]{:S(2)}) async-start(), calls=%async_computation.3 | async-start | bytes 1310720 | tf_op jit(solution)/shard_map/all_gather | solution.py:280
  9.1 97.5 %all-gather.7.cloned.1.call-start = ((), (), s32[]{:S(2)}) async-start(), calls=%async_computation.4 | async-start | bytes 3932160 | tf_op jit(solution)/shard_map/all_gather | solution.py:281
  40.9 231.0 %all-gather.9.cloned.1.call-start = ((), (), s32[]{:S(2)}) async-start(), calls=%async_computation.5 | async-start | bytes 3932160 | tf_op jit(solution)/shard_map/all_gather | solution.py:300
  41.0 36.0 %collective-permute-start.4 = (bf16[512,1536]{1,0:T(8,128)(2,1)}, bf16[512,1536]{1,0:T(8,128)(2,1)}, u32[]{:S(2)}, u32[]{:S(2)}) collective-permute-start(bf16[512,1536]{1,0:T(8,128)(2,1)} %param.17), channel_id=1, source_target_pairs={{0,2},{1,3},{2,0},{3,1},{4,6},{5,7},{6,4},{7,5},{8,10},{9,11},{10,... | collective-permute-start | bytes 4718600 | tf_op jit(solution)/shard_map/ppermute | solution.py:191
  42.5 49.1 %collective-permute-start.9 = (bf16[256,2048]{1,0:T(8,128)(2,1)}, bf16[256,2048]{1,0:T(8,128)(2,1)}, u32[]{:S(2)}, u32[]{:S(2)}) collective-permute-start(bf16[256,2048]{1,0:T(8,128)(2,1)} %all-gather.5.cloned.1.call-done), channel_id=1, source_target_pairs={{0,16},{16,0},{1,17},{17,1},{2,18},{18,2},{3,19},{19,3},{4,20},{20... | collective-permute-start | bytes 3145736 | tf_op jit(solution)/shard_map/ppermute | solution.py:216
  44.0 50.3 %collective-permute-start.3 = (bf16[512,1536]{1,0:T(8,128)(2,1)}, bf16[512,1536]{1,0:T(8,128)(2,1)}, u32[]{:S(2)}, u32[]{:S(2)}) collective-permute-start(bf16[512,1536]{1,0:T(8,128)(2,1)} %param.17), channel_id=1, source_target_pairs={{0,1},{1,0},{2,3},{3,2},{4,5},{5,4},{6,7},{7,6},{8,9},{9,8},{10,11... | collective-permute-start | bytes 4718600 | tf_op jit(solution)/shard_map/ppermute | solution.py:191
  77.0 17.2 %collective-permute-start.5 = (bf16[512,1536]{1,0:T(8,128)(2,1)}, bf16[512,1536]{1,0:T(8,128)(2,1)}, u32[]{:S(2)}, u32[]{:S(2)}) collective-permute-start(bf16[512,1536]{1,0:T(8,128)(2,1)} %collective-permute-done.4), channel_id=1, source_target_pairs={{0,1},{1,0},{2,3},{3,2},{4,5},{5,4},{6,7},{7,6},{8,9},{9,8},{10,11... | collective-permute-start | bytes 4718600 | tf_op jit(solution)/shard_map/ppermute | solution.py:191
  77.8 6.1 collective-permute-start
  79.0 6.4 collective-permute-start.1
  83.9 6.1 collective-permute-start.2
  90.0 47.7 %collective-permute-start.11 = (bf16[512,2048]{1,0:T(8,128)(2,1)}, bf16[512,2048]{1,0:T(8,128)(2,1)}, u32[]{:S(2)}, u32[]{:S(2)}) collective-permute-start(bf16[512,2048]{1,0:T(8,128)(2,1)} %param.23), channel_id=1, source_target_pairs={{0,2},{1,3},{2,0},{3,1},{4,6},{5,7},{6,4},{7,5},{8,10},{9,11},{10,... | collective-permute-start | bytes 6291464 | tf_op jit(solution)/shard_map/ppermute | solution.py:191
  133.9 200.1 %all-gather.11.cloned.1.call-start = ((), (), s32[]{:S(2)}) async-start(), calls=%async_computation.7 | async-start | bytes 3932160 | tf_op jit(solution)/shard_map/all_gather | solution.py:302
  137.7 57.8 %collective-permute-start.12 = (bf16[512,2048]{1,0:T(8,128)(2,1)}, bf16[512,2048]{1,0:T(8,128)(2,1)}, u32[]{:S(2)}, u32[]{:S(2)}) collective-permute-start(bf16[512,2048]{1,0:T(8,128)(2,1)} %get-tuple-element.44), channel_id=1, source_target_pairs={{0,2},{1,3},{2,0},{3,1},{4,6},{5,7},{6,4},{7,5},{8,10},{9,11},{10,... | collective-permute-start | bytes 6291464 | tf_op jit(solution)/shard_map/ppermute | solution.py:191
  140.1 69.9 %collective-permute-start.7 = (bf16[1024,256]{1,0:T(8,128)(2,1)}, bf16[1024,256]{1,0:T(8,128)(2,1)S(1)}, u32[]{:S(2)}, u32[]{:S(2)}) collective-permute-start(bf16[1024,256]{1,0:T(8,128)(2,1)} %get-tuple-element.95), channel_id=1, source_target_pairs={{0,2},{4,3},{8,0},{12,1},{1,6},{5,7},{9,4},{13,5},{2,10},{6,11},{1... | collective-permute-start | bytes 1572872 | tf_op jit(solution)/shard_map/ppermute | solution.py:203
  140.7 69.4 %collective-permute-start.6 = (bf16[1024,256]{1,0:T(8,128)(2,1)S(1)}, bf16[1024,256]{1,0:T(8,128)(2,1)}, u32[]{:S(2)}, u32[]{:S(2)}) collective-permute-start(bf16[1024,256]{1,0:T(8,128)(2,1)S(1)} %get-tuple-element.94), channel_id=1, source_target_pairs={{4,1},{8,2},{12,3},{1,4},{9,6},{13,7},{2,8},{6,9},{14,11},{3,12},{... | collective-permute-start | bytes 1572872 | tf_op jit(solution)/shard_map/ppermute | solution.py:203
  142.1 112.2 %collective-permute-start.14 = (bf16[512,2048]{1,0:T(8,128)(2,1)}, bf16[512,2048]{1,0:T(8,128)(2,1)S(1)}, u32[]{:S(2)}, u32[]{:S(2)}) collective-permute-start(bf16[512,2048]{1,0:T(8,128)(2,1)} %param.23), channel_id=1, source_target_pairs={{0,1},{1,0},{2,3},{3,2},{4,5},{5,4},{6,7},{7,6},{8,9},{9,8},{10,11... | collective-permute-start | bytes 6291464 | tf_op jit(solution)/shard_map/ppermute | solution.py:191
  143.2 120.6 %collective-permute-start.10 = (bf16[512,2048]{1,0:T(8,128)(2,1)}, bf16[512,2048]{1,0:T(8,128)(2,1)}, u32[]{:S(2)}, u32[]{:S(2)}) collective-permute-start(bf16[512,2048]{1,0:T(8,128)(2,1)} %get-tuple-element.44), channel_id=1, source_target_pairs={{0,1},{1,0},{2,3},{3,2},{4,5},{5,4},{6,7},{7,6},{8,9},{9,8},{10,11... | collective-permute-start | bytes 6291464 | tf_op jit(solution)/shard_map/ppermute | solution.py:191
  195.4 58.9 %collective-permute-start.15 = (bf16[512,2048]{1,0:T(8,128)(2,1)}, bf16[512,2048]{1,0:T(8,128)(2,1)}, u32[]{:S(2)}, u32[]{:S(2)}) collective-permute-start(bf16[512,2048]{1,0:T(8,128)(2,1)} %collective-permute-done.11), channel_id=1, source_target_pairs={{0,1},{1,0},{2,3},{3,2},{4,5},{5,4},{6,7},{7,6},{8,9},{9,8},{10,11... | collective-permute-start | bytes 6291464 | tf_op jit(solution)/shard_map/ppermute | solution.py:191
  210.1 53.8 %collective-permute-start.13 = (bf16[512,2048]{1,0:T(8,128)(2,1)}, bf16[512,2048]{1,0:T(8,128)(2,1)}, u32[]{:S(2)}, u32[]{:S(2)}) collective-permute-start(bf16[512,2048]{1,0:T(8,128)(2,1)} %collective-permute-done.12), channel_id=1, source_target_pairs={{0,1},{1,0},{2,3},{3,2},{4,5},{5,4},{6,7},{7,6},{8,9},{9,8},{10,11... | collective-permute-start | bytes 6291464 | tf_op jit(solution)/shard_map/ppermute | solution.py:191
  210.3 25.5 %collective-permute-start.8 = (bf16[2,1024,256]{2,1,0:T(8,128)(2,1)S(1)}, bf16[2,1024,256]{2,1,0:T(8,128)(2,1)S(1)}, u32[]{:S(2)}, u32[]{:S(2)}) collective-permute-start(bf16[2,1024,256]{2,1,0:T(8,128)(2,1)S(1)} %pad_maximum_fusion.5), channel_id=1, source_target_pairs={{0,16},{16,0},{1,17},{17,1},{2,18},{18,2},{3,19},{19,3},{4,20},{20... | collective-permute-start | bytes 3145736 | tf_op jit(solution)/shard_map/ppermute | solution.py:216
  237.5 48.6 %collective-permute-start.17 = (bf16[2,1024,512]{2,1,0:T(8,128)(2,1)}, bf16[2,1024,512]{2,1,0:T(8,128)(2,1)}, u32[]{:S(2)}, u32[]{:S(2)}) collective-permute-start(bf16[2,1024,512]{2,1,0:T(8,128)(2,1)} %pad_maximum_fusion.refs_0_), channel_id=1, source_target_pairs={{0,2},{1,3},{2,0},{3,1},{4,6},{5,7},{6,4},{7,5},{8,10},{9,11},{10,... | collective-permute-start | bytes 6291464 | tf_op jit(solution)/shard_map/ppermute | solution.py:191
  263.5 193.2 %reduce-scatter.4.cloned.1.call-start = ((), (), s32[]{:S(2)}) async-start(), calls=%async_computation.6 | async-start | bytes 7864320 | tf_op jit(solution)/shard_map/reduce_scatter | solution.py:322
  263.8 37.3 %collective-permute-start.16 = (bf16[2,1024,512]{2,1,0:T(8,128)(2,1)}, bf16[2,1024,512]{2,1,0:T(8,128)(2,1)}, u32[]{:S(2)}, u32[]{:S(2)}) collective-permute-start(bf16[2,1024,512]{2,1,0:T(8,128)(2,1)} %pad_maximum_fusion.refs_0_), channel_id=1, source_target_pairs={{0,1},{1,0},{2,3},{3,2},{4,5},{5,4},{6,7},{7,6},{8,9},{9,8},{10,11... | collective-permute-start | bytes 6291464 | tf_op jit(solution)/shard_map/ppermute | solution.py:191
  286.1 15.0 %collective-permute-start.18 = (bf16[2,1024,512]{2,1,0:T(8,128)(2,1)}, bf16[2,1024,512]{2,1,0:T(8,128)(2,1)S(1)}, u32[]{:S(2)}, u32[]{:S(2)}) collective-permute-start(bf16[2,1024,512]{2,1,0:T(8,128)(2,1)} %collective-permute-done.17.refs_2_), channel_id=1, source_target_pairs={{0,1},{1,0},{2,3},{3,2},{4,5},{5,4},{6,7},{7,6},{8,9},{9,8},{10,11... | collective-permute-start | bytes 6291464 | tf_op jit(solution)/shard_map/ppermute | solution.py:191
  325.1 245.0 %reduce-scatter.6.cloned.1.call-start = ((), (), s32[]{:S(2)}) async-start(), calls=%async_computation.8 | async-start | bytes 7864320 | tf_op jit(solution)/shard_map/reduce_scatter | solution.py:342
  367.6 7.5 collective-permute-start.19
  372.7 9.4 %collective-permute-start.20 = (f32[512,2048]{1,0:T(8,128)}, f32[512,2048]{1,0:T(8,128)}, u32[]{:S(2)}, u32[]{:S(2)}) collective-permute-start(f32[512,2048]{1,0:T(8,128)} %fusion.67), channel_id=1, source_target_pairs={{0,1},{1,0},{2,3},{3,2},{4,5},{5,4},{6,7},{7,6},{8,9},{9,8},{10,11... | collective-permute-start | bytes 12582920 | tf_op jit(solution)/shard_map/ppermute | solution.py:191
  456.7 415.9 %reduce-scatter.8.cloned.1.call-start = ((), (), s32[]{:S(2)}) async-start(), calls=%async_computation.9 | async-start | bytes 7864320 | tf_op jit(solution)/shard_map/reduce_scatter | solution.py:360
  462.6 7.5 collective-permute-start.21
  462.6 93.3 %collective-permute-start.22 = (f32[1024,1024]{1,0:T(8,128)}, f32[1024,1024]{1,0:T(8,128)}, u32[]{:S(2)}, u32[]{:S(2)}) collective-permute-start(f32[1024,1024]{1,0:T(8,128)} %convolution_add_fusion.3), channel_id=1, source_target_pairs={{0,2},{1,3},{2,0},{3,1},{4,6},{5,7},{6,4},{7,5},{8,10},{9,11},{10,... | collective-permute-start | bytes 12582920 | tf_op jit(solution)/shard_map/ppermute | solution.py:191
  583.1 9.9 %collective-permute-start.23 = (bf16[192,512]{1,0:T(8,128)(2,1)}, bf16[192,512]{1,0:T(8,128)(2,1)S(1)}, u32[]{:S(2)}, u32[]{:S(2)}) collective-permute-start(bf16[192,512]{1,0:T(8,128)(2,1)} %get-tuple-element.104), channel_id=1, source_target_pairs={{0,4},{4,8},{8,12},{12,0},{1,5},{5,9},{9,13},{13,1},{2,6},{6,10},{... | collective-permute-start | bytes 589832 | tf_op jit(solution)/shard_map/ppermute | solution.py:194
  584.6 15.7 %collective-permute-start.24 = (bf16[192,512]{1,0:T(8,128)(2,1)}, bf16[192,512]{1,0:T(8,128)(2,1)S(1)}, u32[]{:S(2)}, u32[]{:S(2)}) collective-permute-start(bf16[192,512]{1,0:T(8,128)(2,1)} %get-tuple-element.103), channel_id=1, source_target_pairs={{0,8},{4,12},{8,0},{12,4},{1,9},{5,13},{9,1},{13,5},{2,10},{6,14},... | collective-permute-start | bytes 589832 | tf_op jit(solution)/shard_map/ppermute | solution.py:194
  586.3 14.7 %collective-permute-start.25 = (bf16[192,512]{1,0:T(8,128)(2,1)}, bf16[192,512]{1,0:T(8,128)(2,1)S(1)}, u32[]{:S(2)}, u32[]{:S(2)}) collective-permute-start(bf16[192,512]{1,0:T(8,128)(2,1)} %get-tuple-element.102), channel_id=1, source_target_pairs={{0,12},{4,0},{8,4},{12,8},{1,13},{5,1},{9,5},{13,9},{2,14},{6,2},{... | collective-permute-start | bytes 589832 | tf_op jit(solution)/shard_map/ppermute | solution.py:194
  631.4 19.5 %collective-permute-start.26 = (f32[512,1536]{1,0:T(8,128)}, f32[512,1536]{1,0:T(8,128)}, u32[]{:S(2)}, u32[]{:S(2)}) collective-permute-start(f32[512,1536]{1,0:T(8,128)} %fusion.64), channel_id=1, source_target_pairs={{0,1},{1,0},{2,3},{3,2},{4,5},{5,4},{6,7},{7,6},{8,9},{9,8},{10,11... | collective-permute-start | bytes 9437192 | tf_op jit(solution)/shard_map/ppermute | solution.py:191
  636.3 52.3 %collective-permute-start.32 = (f32[512,2048]{1,0:T(8,128)}, f32[512,2048]{1,0:T(8,128)}, u32[]{:S(2)}, u32[]{:S(2)}) collective-permute-start(f32[512,2048]{1,0:T(8,128)} %fusion.57), channel_id=1, source_target_pairs={{0,1},{1,0},{2,3},{3,2},{4,5},{5,4},{6,7},{7,6},{8,9},{9,8},{10,11... | collective-permute-start | bytes 12582920 | tf_op jit(solution)/shard_map/ppermute | solution.py:191
  637.0 92.8 %collective-permute-start.33 = (f32[512,2048]{1,0:T(8,128)}, f32[512,2048]{1,0:T(8,128)}, u32[]{:S(2)}, u32[]{:S(2)}) collective-permute-start(f32[512,2048]{1,0:T(8,128)} %convolution_add_fusion.2), channel_id=1, source_target_pairs={{0,2},{1,3},{2,0},{3,1},{4,6},{5,7},{6,4},{7,5},{8,10},{9,11},{10,... | collective-permute-start | bytes 12582920 | tf_op jit(solution)/shard_map/ppermute | solution.py:191
  639.7 93.8 %collective-permute-start.46 = (f32[2,512]{1,0:T(2,128)S(1)}, f32[2,512]{1,0:T(2,128)S(1)}, u32[]{:S(2)}, u32[]{:S(2)}) collective-permute-start(f32[2,512]{1,0:T(2,128)S(1)} %get-tuple-element.117), channel_id=1, source_target_pairs={{0,12},{4,0},{8,4},{12,8},{1,13},{5,1},{9,5},{13,9},{2,14},{6,2},{... | collective-permute-start | bytes 12296 | tf_op jit(solution)/shard_map/ppermute | solution.py:194
  656.1 30.6 %copy-start.14 = (bf16[768,2048]{1,0:T(8,128)(2,1)S(1)}, bf16[768,2048]{1,0:T(8,128)(2,1)}, u32[]{:S(2)}) copy-start(bf16[768,2048]{1,0:T(8,128)(2,1)} %all-gather.9.cloned.1.call-done) | copy-start | bytes 9437188
  656.3 31.1 %copy-start.17 = (bf16[1024,1024]{1,0:T(8,128)(2,1)S(1)}, bf16[1024,1024]{1,0:T(8,128)(2,1)}, u32[]{:S(2)}) copy-start(bf16[1024,1024]{1,0:T(8,128)(2,1)} %add_convert_fusion.2) | copy-start | bytes 6291460
  656.3 13.8 %collective-permute-start.27 = (bf16[192,512]{1,0:T(8,128)(2,1)S(1)}, bf16[192,512]{1,0:T(8,128)(2,1)S(1)}, u32[]{:S(2)}, u32[]{:S(2)}) collective-permute-start(bf16[192,512]{1,0:T(8,128)(2,1)S(1)} %get-tuple-element.100), channel_id=1, source_target_pairs={{0,4},{4,8},{8,12},{12,0},{1,5},{5,9},{9,13},{13,1},{2,6},{6,10},{... | collective-permute-start | bytes 589832 | tf_op jit(solution)/shard_map/ppermute | solution.py:194
  656.4 26.1 %collective-permute-start.28 = (bf16[192,512]{1,0:T(8,128)(2,1)S(1)}, bf16[192,512]{1,0:T(8,128)(2,1)S(1)}, u32[]{:S(2)}, u32[]{:S(2)}) collective-permute-start(bf16[192,512]{1,0:T(8,128)(2,1)S(1)} %get-tuple-element.99), channel_id=1, source_target_pairs={{0,8},{4,12},{8,0},{12,4},{1,9},{5,13},{9,1},{13,5},{2,10},{6,14},... | collective-permute-start | bytes 589832 | tf_op jit(solution)/shard_map/ppermute | solution.py:194
  670.1 16.5 %collective-permute-start.29 = (bf16[192,512]{1,0:T(8,128)(2,1)S(1)}, bf16[192,512]{1,0:T(8,128)(2,1)S(1)}, u32[]{:S(2)}, u32[]{:S(2)}) collective-permute-start(bf16[192,512]{1,0:T(8,128)(2,1)S(1)} %get-tuple-element.98), channel_id=1, source_target_pairs={{0,12},{4,0},{8,4},{12,8},{1,13},{5,1},{9,5},{13,9},{2,14},{6,2},{... | collective-permute-start | bytes 589832 | tf_op jit(solution)/shard_map/ppermute | solution.py:194
  682.5 184.1 %collective-permute-start.30 = (f32[512,1536]{1,0:T(8,128)}, f32[512,1536]{1,0:T(8,128)}, u32[]{:S(2)}, u32[]{:S(2)}) collective-permute-start(f32[512,1536]{1,0:T(8,128)} %fusion.61), channel_id=1, source_target_pairs={{0,1},{1,0},{2,3},{3,2},{4,5},{5,4},{6,7},{7,6},{8,9},{9,8},{10,11... | collective-permute-start | bytes 9437192 | tf_op jit(solution)/shard_map/ppermute | solution.py:191
  686.7 124.0 %copy-start.4 = (bf16[768,512]{1,0:T(8,128)(2,1)}, bf16[768,512]{1,0:T(8,128)(2,1)S(1)}, u32[]{:S(2)}) copy-start(bf16[768,512]{1,0:T(8,128)(2,1)S(1)} %constant_dynamic-update-slice_fusion) | copy-start | bytes 2359300
  687.4 118.4 %collective-permute-start.42 = (f32[512,512]{1,0:T(8,128)S(1)}, f32[512,512]{1,0:T(8,128)S(1)}, u32[]{:S(2)}, u32[]{:S(2)}) collective-permute-start(f32[512,512]{1,0:T(8,128)S(1)} %fusion.51), channel_id=1, source_target_pairs={{0,1},{1,0},{2,3},{3,2},{4,5},{5,4},{6,7},{7,6},{8,9},{9,8},{10,11... | collective-permute-start | bytes 3145736 | tf_op jit(solution)/shard_map/ppermute | solution.py:191
  688.7 47.8 %collective-permute-start.39 = (f32[1536]{0:T(1024)S(1)}, f32[1536]{0:T(1024)S(1)}, u32[]{:S(2)}, u32[]{:S(2)}) collective-permute-start(f32[1536]{0:T(1024)S(1)} %convert_reduce_fusion.3), channel_id=1, source_target_pairs={{0,1},{1,0},{2,3},{3,2},{4,5},{5,4},{6,7},{7,6},{8,9},{9,8},{10,11... | collective-permute-start | bytes 18440 | tf_op jit(solution)/shard_map/ppermute | solution.py:191
  729.8 93.9 %collective-permute-start.50 = (bf16[1024,512]{1,0:T(8,128)(2,1)S(1)}, bf16[1024,512]{1,0:T(8,128)(2,1)S(1)}, u32[]{:S(2)}, u32[]{:S(2)}) collective-permute-start(bf16[1024,512]{1,0:T(8,128)(2,1)S(1)} %get-tuple-element.85), channel_id=1, source_target_pairs={{0,8},{4,9},{8,10},{12,11},{1,12},{5,13},{9,14},{13,15},{2,0},{6,1... | collective-permute-start | bytes 3145736 | tf_op jit(solution)/shard_map/ppermute | solution.py:203
  733.5 133.2 %collective-permute-start.31 = (f32[512,1536]{1,0:T(8,128)}, f32[512,1536]{1,0:T(8,128)}, u32[]{:S(2)}, u32[]{:S(2)}) collective-permute-start(f32[512,1536]{1,0:T(8,128)} %convolution_add_fusion.1), channel_id=1, source_target_pairs={{0,2},{1,3},{2,0},{3,1},{4,6},{5,7},{6,4},{7,5},{8,10},{9,11},{10,... | collective-permute-start | bytes 9437192 | tf_op jit(solution)/shard_map/ppermute | solution.py:191
  736.5 35.6 %collective-permute-start.45 = (f32[2,512]{1,0:T(2,128)S(1)}, f32[2,512]{1,0:T(2,128)S(1)}, u32[]{:S(2)}, u32[]{:S(2)}) collective-permute-start(f32[2,512]{1,0:T(2,128)S(1)} %get-tuple-element.116), channel_id=1, source_target_pairs={{0,8},{4,12},{8,0},{12,4},{1,9},{5,13},{9,1},{13,5},{2,10},{6,14},... | collective-permute-start | bytes 12296 | tf_op jit(solution)/shard_map/ppermute | solution.py:194
  772.2 32.9 %collective-permute-start.44 = (f32[2,512]{1,0:T(2,128)S(1)}, f32[2,512]{1,0:T(2,128)S(1)}, u32[]{:S(2)}, u32[]{:S(2)}) collective-permute-start(f32[2,512]{1,0:T(2,128)S(1)} %get-tuple-element.115), channel_id=1, source_target_pairs={{0,4},{4,8},{8,12},{12,0},{1,5},{5,9},{9,13},{13,1},{2,6},{6,10},{... | collective-permute-start | bytes 12296 | tf_op jit(solution)/shard_map/ppermute | solution.py:194
  805.0 25.8 %collective-permute-start.49 = (bf16[1024,512]{1,0:T(8,128)(2,1)}, bf16[1024,512]{1,0:T(8,128)(2,1)S(1)}, u32[]{:S(2)}, u32[]{:S(2)}) collective-permute-start(bf16[1024,512]{1,0:T(8,128)(2,1)} %get-tuple-element.84), channel_id=1, source_target_pairs={{4,1},{8,2},{12,3},{1,4},{9,6},{13,7},{2,8},{6,9},{14,11},{3,12},{... | collective-permute-start | bytes 3145736 | tf_op jit(solution)/shard_map/ppermute | solution.py:203
  805.8 17.9 %collective-permute-start.40 = (f32[1536]{0:T(1024)S(1)}, f32[1536]{0:T(1024)S(1)}, u32[]{:S(2)}, u32[]{:S(2)}) collective-permute-start(f32[1536]{0:T(1024)S(1)} %add.454), channel_id=1, source_target_pairs={{0,2},{1,3},{2,0},{3,1},{4,6},{5,7},{6,4},{7,5},{8,10},{9,11},{10,... | collective-permute-start | bytes 18440 | tf_op jit(solution)/shard_map/ppermute | solution.py:191
  823.7 10.3 %collective-permute-start.41 = (f32[512,512]{1,0:T(8,128)}, f32[512,512]{1,0:T(8,128)S(1)}, u32[]{:S(2)}, u32[]{:S(2)}) collective-permute-start(f32[512,512]{1,0:T(8,128)} %fusion.54), channel_id=1, source_target_pairs={{0,1},{1,0},{2,3},{3,2},{4,5},{5,4},{6,7},{7,6},{8,9},{9,8},{10,11... | collective-permute-start | bytes 3145736 | tf_op jit(solution)/shard_map/ppermute | solution.py:191
  823.7 40.4 %collective-permute-start.43 = (f32[512,512]{1,0:T(8,128)}, f32[512,512]{1,0:T(8,128)S(1)}, u32[]{:S(2)}, u32[]{:S(2)}) collective-permute-start(f32[512,512]{1,0:T(8,128)} %convolution_add_fusion.4), channel_id=1, source_target_pairs={{0,2},{1,3},{2,0},{3,1},{4,6},{5,7},{6,4},{7,5},{8,10},{9,11},{10,... | collective-permute-start | bytes 3145736 | tf_op jit(solution)/shard_map/ppermute | solution.py:191
  832.6 31.6 %copy-start.5 = (bf16[768,512]{1,0:T(8,128)(2,1)S(1)}, bf16[768,512]{1,0:T(8,128)(2,1)}, u32[]{:S(2)}) copy-start(bf16[768,512]{1,0:T(8,128)(2,1)} %copy-done.4) | copy-start | bytes 2359300
  834.0 32.6 %copy-start.3 = (bf16[768,1536]{1,0:T(8,128)(2,1)S(1)}, bf16[768,1536]{1,0:T(8,128)(2,1)}, u32[]{:S(2)}) copy-start(bf16[768,1536]{1,0:T(8,128)(2,1)} %attn_bwd.1) | copy-start | bytes 7077892
  875.2 4.2 collective-permute-start.37
  875.3 4.5 collective-permute-start.36
  877.5 4.5 collective-permute-start.35
  877.5 5.4 collective-permute-start.34
  879.4 5.3 collective-permute-start.38
  884.6 1.2 collective-permute-start.47
  885.9 3.7 collective-permute-start.48
  (26 other events, 165.4 us)
Sparse Core Ops, SparseCore 0:
  10.1 30.6 all-gather.4
  42.5 64.1 all-gather.6
  134.0 103.5 all-gather.8
  263.6 70.3 all-gather.10
  336.1 120.4 reduce-scatter.3
  458.8 111.2 reduce-scatter.5
  626.5 140.3 reduce-scatter.7

commit v3 on v2

--- a/solution.py
+++ b/solution.py
@@ -350,6 +350,7 @@
         gin = inv_t * (ghat - jnp.mean(ghat, axis=-1, keepdims=True) - hat_t * jnp.mean(ghat * hat_t, axis=-1, keepdims=True))
         gr_tok = (col_block(g_full, 0, col, tok_local).astype(F32) + gin).astype(BF16)
         grad_attn = spread(dot_nt(gr_tok, wo).astype(BF16))
+        gr_mine = spread(tie(gr_tok, grad_attn))
         wout_even = cross_even(col_block(tie(wout_sum, grad_attn), 1, near_y, d_local))
         wout_odd = cross(col_block(tie(wout_sum, grad_attn), 1, 1 - near_y, d_local), lambda r, c: (c, r ^ 2))
         grad_qkv = attn_backward(qkv_rows, grad_attn, attn_stats, head_dim)
@@ -362,14 +363,16 @@
         make_wqkv = lambda j: dot_tn(col_block(h1_l, 1, j, k_local), gq_l)
         wqkv_send, wqkv_own = scatter_near(make_wqkv)
         wqkv_far = flip_row(wqkv_send, 2)
-        gr_mine = spread(tie(gr_tok, wqkv_send))
-        make_wo = lambda j: dot_tn(col_block(attn_full, 1, j, k_local), gr_mine)
+        gr_l = tie(gr_mine, wqkv_send)
+        make_wo = lambda j: dot_tn(col_block(attn_full, 1, j, k_local), gr_l)
         wo_send, wo_own = scatter_near(make_wo)
         gwo_far = flip_row(wo_send, 2)
         grad_wqkv = scatter_far(make_wqkv, wqkv_own, wqkv_far)
         grad_win = scatter_far(make_win, win_own, win_far)
         grad_wo = scatter_far(make_wo, wo_own, gwo_far)
-        gn1 = tie(gn1, grad_wqkv, grad_win).astype(BF16).astype(F32)
+        gs2 = tie(gs2, gn1)
+        gn1_raw = gn1
+        gn1 = tie(gn1, grad_win).astype(BF16).astype(F32)
         hat1 = (x_rows.astype(F32) - mean1) * inv1
         ghat1 = gn1 * ln1_scale
         sums = jnp.stack([jnp.sum(ghat1, axis=-1), jnp.sum(ghat1 * hat1, axis=-1)])
@@ -383,11 +386,10 @@
         ln2_part = col_block(gs2, 1, col, d_local)
         for step in range(1, n_col):
             ln2_part = ln2_part + shift_col(col_block(gs2, 1, (col + step) % n_col, d_local), step)
-        early = sum_row(jnp.concatenate([ln2_part.reshape(-1), tok_sum(grad_rows), tok_sum(gr_mine), tok_sum(grad_pre)]))
-        gl2s, gl2t, gbout, gbo, gbin = jnp.split(early, [d_local * k for k in range(1, 5)])
-        gbqkv = sum_row(tok_sum(grad_qkv))
-        late = sum_row(jnp.stack([jnp.sum(gn1 * hat1, axis=0), jnp.sum(gn1, axis=0)]))
-        return (out_rows.reshape(x_blk.shape), grad_x.reshape(x_blk.shape), late[0], late[1], grad_wqkv, gbqkv.reshape(heads_local, qkv_width), grad_wo, gbo, gl2s, gl2t, grad_win, gbin, grad_wout, gbout)
+        sums_early = tie(jnp.concatenate([tok_sum(grad_rows), tok_sum(gr_mine), tok_sum(grad_pre), tok_sum(grad_qkv)]), gn1_raw)
+        small = sum_row(jnp.concatenate([ln2_part.reshape(-1), jnp.sum(gn1 * hat1, axis=0), jnp.sum(gn1, axis=0), sums_early]))
+        gl2s, gl2t, gl1s, gl1t, gbout, gbo, gbin, gbqkv = jnp.split(small, [d_local * k for k in (1, 2, 3, 4, 5, 6, 6 + n_col)])
+        return (out_rows.reshape(x_blk.shape), grad_x.reshape(x_blk.shape), gl1s, gl1t, grad_wqkv, gbqkv.reshape(heads_local, qkv_width), grad_wo, gbo, gl2s, gl2t, grad_win, gbin, grad_wout, gbout)
 
     return jax.shard_map(layer_block, mesh=mesh,
                          in_specs=(act_spec, vec_spec, vec_spec, mat_spec, head_spec, mat_spec, vec_spec, vec_spec, vec_spec, mat_spec, vec_spec, mat_spec, vec_spec, act_spec),

time: 907 us -> 925 us (1.020)
  waiting for transfers between devices: 509 us -> 566 us
  starting transfers between devices: 97.2 us -> 66 us
    ppermute x30 -> x26, waiting for transfers between devices: 268 us -> 328 us  [flip_row(): return lax.ppermute(val, 'row', [(src, src ^ bits) for src in range(n_row)])]
    ppermute x15, starting transfers between devices: 53.6 us -> 26.4 us  [shift_col(): lax.ppermute(val, 'col', [(src, (src + step) % n_col) for src in range(n_...]
    ppermute x30 -> x26, starting transfers between devices: 33.3 us -> 29.9 us  [flip_row(): return lax.ppermute(val, 'row', [(src, src ^ bits) for src in range(n_row)])]
  transfers between devices with their start and end apart: 58 -> 54, of which waited for: 29 -> 24; matrix products, arithmetic and copies ran while one was open for 20% -> 19% of each run, Pallas kernels for 5% -> 5%
where the time goes in v3:
time: 925 us; the launch traced here: 917 us
  waiting for transfers between devices  566 us (61%)
  matrix products  154 us (17%)
  starting transfers between devices  66 us (7%)
  Pallas kernels  60.4 us (7%)
  other arithmetic  35.8 us (4%)
  local copies, waits for them, and re-layouts  19.1 us (2%)
  between operations  15.4 us (2%)
    ppermute x26, waiting for transfers between devices, flip_row(): return lax.ppermute(val, 'row', [(src, src ^ bits) for src in range(n_row)])  328 us
    ppermute x15, waiting for transfers between devices, shift_col(): lax.ppermute(val, 'col', [(src, (src + step) % n_col) for src in range(n_...  78.6 us
    reduce_scatter x1, waiting for transfers between devices, layer_block(): out_part = lax.psum_scatter(out_dot, 'col', scatter_dimension=1, tiled=True)  68.3 us
    dot_general x16, matrix products, dot_tn(): lax.dot_general(lhs, rhs, (((0,), (0,)), ((), ())), preferred_element_typ...  66.8 us
    dot_general x4, matrix products, dot_nn(): return jnp.dot(lhs, rhs, preferred_element_type=F32)  44.4 us
    dot_general x4, matrix products, dot_nt(): lax.dot_general(lhs, rhs, (((1,), (1,)), ((), ())), preferred_element_typ...  42.8 us
    pallas_call x4, Pallas kernels, place_blocks(): pl.pallas_call(functools.partial(place_kernel, count), grid_spec=pltpu.Pr...  33.3 us
    all_gather x1, waiting for transfers between devices, layer_block(): wo_half = lax.all_gather(half_dp(w_o, 0), 'col', axis=1, tiled=True)  31.8 us
  transfers between devices with their start and end apart: 54, of which 24 were waited for; matrix products, arithmetic and copies ran while one was open for 19% of the time, Pallas kernels for 5%

profile of v3, /device:TPU:0, one launch (start us, length us, event | category | flops | bytes accessed | tf_op | source)
XLA Modules:
  0.0 916.8 jit_solution(10255037995539788308)
XLA Ops:
  9.1 31.8 %all-gather.5.cloned.1.call-done = bf16[256,2048]{1,0:T(8,128)(2,1)} async-done(((bf16[256,512]{1,0:T(8,128)(2,1)}), bf16[256,2048]{1,0:T(8,128)(2,1)}) %all-gather.5.cloned.1.call-update) | async-done | bytes 1048592 | tf_op jit(solution)/shard_map/all_gather | solution.py:280
  44.0 33.0 %collective-permute-done.4 = bf16[512,1536]{1,0:T(8,128)(2,1)} collective-permute-done((bf16[512,1536]{1,0:T(8,128)(2,1)}, bf16[512,1536]{1,0:T(8,128)(2,1)}, u32[]{:S(2)}, u32[]{:S(2)}) %collective-permute-start.4) | collective-permute-done | bytes 1572896 | tf_op jit(solution)/shard_map/ppermute | solution.py:191
  85.4 4.6 collective-permute-done.2
  91.6 2.7 broadcast_select_fusion.4
  94.2 6.6 place_blocks.4
  100.8 5.8 all-gather.7.cloned.1.call-done
  106.6 3.0 convert_reduce_fusion
  109.7 2.8 fusion.18
  113.6 8.2 add_convert_fusion.qkv_ref
  121.9 12.0 %attn_fwd.1 = (bf16[768,512]{1,0:T(8,128)(2,1)}, f32[4,8,768]{2,1,0:T(8,128)}) custom-call(bf16[768,1536]{1,0:T(8,128)(2,1)} %add_convert_fusion.qkv_ref), custom_call_target="tpu_custom_call" | custom-call | flops 1207959552 | bytes 4718592 | tf_op jit(solution)/shard_map/attn_fwd/pallas_call | solution.py:111
  133.9 3.8 pad_maximum_fusion.1
  143.3 52.1 %collective-permute-done.12 = bf16[512,2048]{1,0:T(8,128)(2,1)} collective-permute-done((bf16[512,2048]{1,0:T(8,128)(2,1)}, bf16[512,2048]{1,0:T(8,128)(2,1)}, u32[]{:S(2)}, u32[]{:S(2)}) %collective-permute-start.12) | collective-permute-done | bytes 2097184 | tf_op jit(solution)/shard_map/ppermute | solution.py:191
  195.5 14.6 %collective-permute-done.7 = bf16[1024,256]{1,0:T(8,128)(2,1)S(1)} collective-permute-done((bf16[1024,256]{1,0:T(8,128)(2,1)}, bf16[1024,256]{1,0:T(8,128)(2,1)S(1)}, u32[]{:S(2)}, u32[]{:S(2)}) %collective-permute-start.7) | collective-permute-done | bytes 524320 | tf_op jit(solution)/shard_map/ppermute | solution.py:203
  211.9 24.0 %collective-permute-done.8 = bf16[2,1024,256]{2,1,0:T(8,128)(2,1)S(1)} collective-permute-done((bf16[2,1024,256]{2,1,0:T(8,128)(2,1)S(1)}, bf16[2,1024,256]{2,1,0:T(8,128)(2,1)S(1)}, u32[]{:S(2)}, u32[]{:S(2)}) %collective-permute-start.8) | collective-permute-done | bytes 1048608 | tf_op jit(solution)/shard_map/ppermute | solution.py:216
  237.5 16.3 %collective-permute-start.17 = (bf16[2,1024,512]{2,1,0:T(8,128)(2,1)}, bf16[2,1024,512]{2,1,0:T(8,128)(2,1)}, u32[]{:S(2)}, u32[]{:S(2)}) collective-permute-start(bf16[2,1024,512]{2,1,0:T(8,128)(2,1)} %pad_maximum_fusion.refs_0_), channel_id=1, source_target_pairs={{0,2},{1,3},{2,0},{3,1},{4,6},{5,7},{6,4},{7,5},{8,10},{9,11},{10,... | collective-permute-start | bytes 6291464 | tf_op jit(solution)/shard_map/ppermute | solution.py:191
  255.7 7.8 place_blocks.6
  263.9 8.0 place_blocks.5
  272.0 10.6 %convert_reduce_fusion.1 = (f32[768]{0:T(1024)S(1)}, f32[768]{0:T(1024)S(1)}, bf16[768,2048]{1,0:T(8,128)(2,1)S(1)}) fusion(f32[2048]{0:T(1024)S(1)} %bitcast.95, bf16[768,2048]{1,0:T(8,128)(2,1)} %all-gather.9.cloned.1.call-done, bf16[2048,2048]{1,0:T(8,128)(2,1)} %place_blocks.5, bf16[768,2048]{1,0:T(8,128)(2,1)S(1)} %copy-done.6), kind=kOutput, calls=%fused_computation.6 | convolution fusion | flops 6455031808 | bytes 17840128 | tf_op jit(solution)/shard_map/dot_general | solution.py:23
  282.6 3.6 collective-permute-done.17.refs_2_
  287.5 13.7 %multiply_convert_fusion = (bf16[768,2048]{1,0:T(8,128)(2,1)}, f32[768,2048]{1,0:T(8,128)}) fusion(f32[2048]{0:T(1024)S(1)} %copy-done.28, bf16[768,2048]{1,0:T(8,128)(2,1)S(1)} %fusion.13, bf16[2048,2048]{1,0:T(8,128)(2,1)} %place_blocks.6), kind=kOutput, calls=%fused_computation.34 | convolution fusion | flops 6458179584 | bytes 20979712 | tf_op jit(solution)/shard_map/dot_general | solution.py:23
  302.5 10.9 %place_blocks.7 = bf16[2048,2048]{1,0:T(8,128)(2,1)} custom-call(s32[16]{0:T(128)} %stack.121.index_ref, bf16[2,1024,512]{2,1,0:T(8,128)(2,1)} %pad_maximum_fusion.refs_0_, bf16[2,1024,512]{2,1,0:T(8,128)(2,1)} %collective-permute-done.16.refs_1_, bf16[2,1024,512]{2,1,0:T(8,128)(2,1)} %collective-permute-done.17.refs_2_, bf16[2,1024,512]{2,1,0:T(8,128)(2,1)} %copy-done.15), custom_call_target="tpu_custom_call" | custom-call | flops 40000000 | bytes 16777216 | tf_op jit(solution)/shard_map/place_blocks/pallas_call | solution.py:160
  313.3 11.8 %fusion.98 = f32[768,2048]{1,0:T(8,128)} fusion(bf16[768,2048]{1,0:T(8,128)(2,1)} %get-tuple-element.52, bf16[2048,2048]{1,0:T(8,128)(2,1)} %place_blocks.7), kind=kOutput, calls=%fused_computation.196 | convolution fusion | flops 6442450944 | bytes 17825792 | tf_op jit(solution)/shard_map/dot_general | solution.py:23
  325.5 8.5 all-gather.11.cloned.1.call-done
  334.0 15.3 %convert_reduce_fusion.2 = (f32[2048]{0:T(1024)}, bf16[768,2048]{1,0:T(8,128)(2,1)S(1)}) fusion(f32[768,2048]{1,0:T(8,128)} %get-tuple-element.132, f32[2048]{0:T(1024)S(1)} %copy-done.28, bf16[768,2048]{1,0:T(8,128)(2,1)} %all-gather.11.cloned.1.call-done, bf16[2048,2048]{1,0:T(8,128)(2,1)} %place_blocks.7), kind=kOutput, calls=%fused_computation.33 | convolution fusion | flops 6481770496 | bytes 20987904 | tf_op jit(solution)/shard_map/dot_general | solution.py:27
  349.3 11.3 %fusion.99 = f32[768,2048]{1,0:T(8,128)} fusion(bf16[768,2048]{1,0:T(8,128)(2,1)S(1)} %get-tuple-element.55, bf16[2048,2048]{1,0:T(8,128)(2,1)} %place_blocks.6), kind=kOutput, calls=%fused_computation.197 | convolution fusion | flops 6442450944 | bytes 17825792 | tf_op jit(solution)/shard_map/dot_general | solution.py:27
  360.6 3.4 constant_dynamic-slice_fusion.14
  364.0 3.8 fusion.44
  367.8 5.0 fusion.67
  375.3 6.9 convolution_add_fusion.3
  382.2 6.3 convolution_add_fusion.2
  388.5 68.3 %reduce-scatter.4.cloned.1.call-done = f32[768,512]{1,0:T(8,128)} async-done(((f32[768,2048]{1,0:T(8,128)}), f32[768,512]{1,0:T(8,128)}) %reduce-scatter.4.cloned.1.call-update) | async-done | bytes 1572880 | tf_op jit(solution)/shard_map/reduce_scatter | solution.py:322
  457.1 5.7 fusion.41
  464.4 5.9 collective-permute-done.21
  470.3 85.8 %collective-permute-done.22 = f32[1024,1024]{1,0:T(8,128)} collective-permute-done((f32[1024,1024]{1,0:T(8,128)}, f32[1024,1024]{1,0:T(8,128)}, u32[]{:S(2)}, u32[]{:S(2)}) %collective-permute-start.22) | collective-permute-done | bytes 4194336 | tf_op jit(solution)/shard_map/ppermute | solution.py:191
  556.1 7.5 add_convert_fusion.2
  563.6 6.7 reduce-scatter.6.cloned.1.call-done
  570.3 2.5 fusion.39
  572.8 2.1 fusion.37
  575.0 6.6 convolution_convert_fusion.1
  586.5 2.9 collective-permute-start.25
  589.4 3.9 collective-permute-done.23
  594.0 6.5 collective-permute-done.24
  601.9 15.1 %attn_bwd.1 = bf16[768,1536]{1,0:T(8,128)(2,1)} custom-call(bf16[768,1536]{1,0:T(8,128)(2,1)} %add_convert_fusion.qkv_ref, bf16[768,512]{1,0:T(8,128)(2,1)} %constant_dynamic-update-slice_fusion.3.grad_ref, f32[4,8,768]{2,1,0:T(8,128)} %get-tuple-element.59.stat_ref), custom_call_target="tpu_custom_call" | custom-call | flops 3019898880 | bytes 4718592 | tf_op jit(solution)/shard_map/attn_bwd/pallas_call | solution.py:125
  617.0 9.7 %fusion.100 = f32[768,2048]{1,0:T(8,128)} fusion(bf16[768,1536]{1,0:T(8,128)(2,1)} %attn_bwd.1, bf16[2048,1536]{1,0:T(8,128)(2,1)} %place_blocks.4), kind=kOutput, calls=%fused_computation.198 | convolution fusion | flops 4831838208 | bytes 14942208 | tf_op jit(solution)/shard_map/dot_general | solution.py:27
  626.7 5.0 fusion.63
  634.4 3.3 fusion.57
  638.1 3.2 fusion.65
  641.3 2.3 fusion.49
  643.7 81.3 %collective-permute-done.30 = f32[512,2048]{1,0:T(8,128)} collective-permute-done((f32[512,2048]{1,0:T(8,128)}, f32[512,2048]{1,0:T(8,128)}, u32[]{:S(2)}, u32[]{:S(2)}) %collective-permute-start.30) | collective-permute-done | bytes 4194336 | tf_op jit(solution)/shard_map/ppermute | solution.py:191
  724.9 6.0 add_convert_fusion.1
  731.2 3.1 collective-permute-start.46
  735.2 6.3 collective-permute-start.26
  742.6 4.2 fusion.60
  747.2 34.9 %collective-permute-done.26 = bf16[192,512]{1,0:T(8,128)(2,1)S(1)} collective-permute-done((bf16[192,512]{1,0:T(8,128)(2,1)S(1)}, bf16[192,512]{1,0:T(8,128)(2,1)S(1)}, u32[]{:S(2)}, u32[]{:S(2)}) %collective-permute-start.26) | collective-permute-done | bytes 196640 | tf_op jit(solution)/shard_map/ppermute | solution.py:194
  782.1 15.0 %collective-permute-done.27 = bf16[192,512]{1,0:T(8,128)(2,1)S(1)} collective-permute-done((bf16[192,512]{1,0:T(8,128)(2,1)S(1)}, bf16[192,512]{1,0:T(8,128)(2,1)S(1)}, u32[]{:S(2)}, u32[]{:S(2)}) %collective-permute-start.27) | collective-permute-done | bytes 196640 | tf_op jit(solution)/shard_map/ppermute | solution.py:194
  798.0 4.4 collective-permute-done.28
  802.6 4.5 convolution_add_fusion
  807.1 2.1 collective-permute-start.41
  813.0 2.4 fusion.40
  815.4 2.7 collective-permute-start.36
  826.0 2.1 collective-permute-done.34
  828.4 5.4 collective-permute-done.31
  835.6 63.9 %collective-permute-done.44 = f32[512,512]{1,0:T(8,128)S(1)} collective-permute-done((f32[512,512]{1,0:T(8,128)S(1)}, f32[512,512]{1,0:T(8,128)S(1)}, u32[]{:S(2)}, u32[]{:S(2)}) %collective-permute-start.44) | collective-permute-done | bytes 1048608 | tf_op jit(solution)/shard_map/ppermute | solution.py:191
  901.7 5.9 fusion.23
  (207 shorter events, 66.1 us)
Async XLA Ops:
  7.2 132.0 %copy-start = (bf16[2048,512]{1,0:T(8,128)(2,1)S(1)}, bf16[2048,512]{1,0:T(8,128)(2,1)}, u32[]{:S(2)}) copy-start(bf16[2048,512]{1,0:T(8,128)(2,1)} %param.25) | copy-start | bytes 6291460
  7.2 33.7 %all-gather.5.cloned.1.call-start = ((), (), s32[]{:S(2)}) async-start(), calls=%async_computation.3 | async-start | bytes 1310720 | tf_op jit(solution)/shard_map/all_gather | solution.py:280
  9.1 97.5 %all-gather.7.cloned.1.call-start = ((), (), s32[]{:S(2)}) async-start(), calls=%async_computation.4 | async-start | bytes 3932160 | tf_op jit(solution)/shard_map/all_gather | solution.py:281
  40.9 231.1 %all-gather.9.cloned.1.call-start = ((), (), s32[]{:S(2)}) async-start(), calls=%async_computation.5 | async-start | bytes 3932160 | tf_op jit(solution)/shard_map/all_gather | solution.py:300
  41.0 36.0 %collective-permute-start.4 = (bf16[512,1536]{1,0:T(8,128)(2,1)}, bf16[512,1536]{1,0:T(8,128)(2,1)}, u32[]{:S(2)}, u32[]{:S(2)}) collective-permute-start(bf16[512,1536]{1,0:T(8,128)(2,1)} %param.17), channel_id=1, source_target_pairs={{0,2},{1,3},{2,0},{3,1},{4,6},{5,7},{6,4},{7,5},{8,10},{9,11},{10,... | collective-permute-start | bytes 4718600 | tf_op jit(solution)/shard_map/ppermute | solution.py:191
  42.5 49.1 %collective-permute-start.9 = (bf16[256,2048]{1,0:T(8,128)(2,1)}, bf16[256,2048]{1,0:T(8,128)(2,1)}, u32[]{:S(2)}, u32[]{:S(2)}) collective-permute-start(bf16[256,2048]{1,0:T(8,128)(2,1)} %all-gather.5.cloned.1.call-done), channel_id=1, source_target_pairs={{0,16},{16,0},{1,17},{17,1},{2,18},{18,2},{3,19},{19,3},{4,20},{20... | collective-permute-start | bytes 3145736 | tf_op jit(solution)/shard_map/ppermute | solution.py:216
  44.0 50.3 %collective-permute-start.3 = (bf16[512,1536]{1,0:T(8,128)(2,1)}, bf16[512,1536]{1,0:T(8,128)(2,1)}, u32[]{:S(2)}, u32[]{:S(2)}) collective-permute-start(bf16[512,1536]{1,0:T(8,128)(2,1)} %param.17), channel_id=1, source_target_pairs={{0,1},{1,0},{2,3},{3,2},{4,5},{5,4},{6,7},{7,6},{8,9},{9,8},{10,11... | collective-permute-start | bytes 4718600 | tf_op jit(solution)/shard_map/ppermute | solution.py:191
  77.0 17.2 %collective-permute-start.5 = (bf16[512,1536]{1,0:T(8,128)(2,1)}, bf16[512,1536]{1,0:T(8,128)(2,1)}, u32[]{:S(2)}, u32[]{:S(2)}) collective-permute-start(bf16[512,1536]{1,0:T(8,128)(2,1)} %collective-permute-done.4), channel_id=1, source_target_pairs={{0,1},{1,0},{2,3},{3,2},{4,5},{5,4},{6,7},{7,6},{8,9},{9,8},{10,11... | collective-permute-start | bytes 4718600 | tf_op jit(solution)/shard_map/ppermute | solution.py:191
  77.8 6.1 collective-permute-start
  79.0 6.4 collective-permute-start.1
  83.9 6.1 collective-permute-start.2
  90.0 47.7 %collective-permute-start.11 = (bf16[512,2048]{1,0:T(8,128)(2,1)}, bf16[512,2048]{1,0:T(8,128)(2,1)}, u32[]{:S(2)}, u32[]{:S(2)}) collective-permute-start(bf16[512,2048]{1,0:T(8,128)(2,1)} %param.23), channel_id=1, source_target_pairs={{0,2},{1,3},{2,0},{3,1},{4,6},{5,7},{6,4},{7,5},{8,10},{9,11},{10,... | collective-permute-start | bytes 6291464 | tf_op jit(solution)/shard_map/ppermute | solution.py:191
  133.9 200.1 %all-gather.11.cloned.1.call-start = ((), (), s32[]{:S(2)}) async-start(), calls=%async_computation.7 | async-start | bytes 3932160 | tf_op jit(solution)/shard_map/all_gather | solution.py:302
  137.7 57.8 %collective-permute-start.12 = (bf16[512,2048]{1,0:T(8,128)(2,1)}, bf16[512,2048]{1,0:T(8,128)(2,1)}, u32[]{:S(2)}, u32[]{:S(2)}) collective-permute-start(bf16[512,2048]{1,0:T(8,128)(2,1)} %get-tuple-element.47), channel_id=1, source_target_pairs={{0,2},{1,3},{2,0},{3,1},{4,6},{5,7},{6,4},{7,5},{8,10},{9,11},{10,... | collective-permute-start | bytes 6291464 | tf_op jit(solution)/shard_map/ppermute | solution.py:191
  140.1 70.0 %collective-permute-start.7 = (bf16[1024,256]{1,0:T(8,128)(2,1)}, bf16[1024,256]{1,0:T(8,128)(2,1)S(1)}, u32[]{:S(2)}, u32[]{:S(2)}) collective-permute-start(bf16[1024,256]{1,0:T(8,128)(2,1)} %get-tuple-element.101), channel_id=1, source_target_pairs={{0,2},{4,3},{8,0},{12,1},{1,6},{5,7},{9,4},{13,5},{2,10},{6,11},{1... | collective-permute-start | bytes 1572872 | tf_op jit(solution)/shard_map/ppermute | solution.py:203
  140.7 69.4 %collective-permute-start.6 = (bf16[1024,256]{1,0:T(8,128)(2,1)S(1)}, bf16[1024,256]{1,0:T(8,128)(2,1)}, u32[]{:S(2)}, u32[]{:S(2)}) collective-permute-start(bf16[1024,256]{1,0:T(8,128)(2,1)S(1)} %get-tuple-element.100), channel_id=1, source_target_pairs={{4,1},{8,2},{12,3},{1,4},{9,6},{13,7},{2,8},{6,9},{14,11},{3,12},{... | collective-permute-start | bytes 1572872 | tf_op jit(solution)/shard_map/ppermute | solution.py:203
  142.2 112.2 %collective-permute-start.14 = (bf16[512,2048]{1,0:T(8,128)(2,1)}, bf16[512,2048]{1,0:T(8,128)(2,1)S(1)}, u32[]{:S(2)}, u32[]{:S(2)}) collective-permute-start(bf16[512,2048]{1,0:T(8,128)(2,1)} %param.23), channel_id=1, source_target_pairs={{0,1},{1,0},{2,3},{3,2},{4,5},{5,4},{6,7},{7,6},{8,9},{9,8},{10,11... | collective-permute-start | bytes 6291464 | tf_op jit(solution)/shard_map/ppermute | solution.py:191
  143.2 120.7 %collective-permute-start.10 = (bf16[512,2048]{1,0:T(8,128)(2,1)}, bf16[512,2048]{1,0:T(8,128)(2,1)}, u32[]{:S(2)}, u32[]{:S(2)}) collective-permute-start(bf16[512,2048]{1,0:T(8,128)(2,1)} %get-tuple-element.47), channel_id=1, source_target_pairs={{0,1},{1,0},{2,3},{3,2},{4,5},{5,4},{6,7},{7,6},{8,9},{9,8},{10,11... | collective-permute-start | bytes 6291464 | tf_op jit(solution)/shard_map/ppermute | solution.py:191
  195.5 59.0 %collective-permute-start.15 = (bf16[512,2048]{1,0:T(8,128)(2,1)}, bf16[512,2048]{1,0:T(8,128)(2,1)}, u32[]{:S(2)}, u32[]{:S(2)}) collective-permute-start(bf16[512,2048]{1,0:T(8,128)(2,1)} %collective-permute-done.11), channel_id=1, source_target_pairs={{0,1},{1,0},{2,3},{3,2},{4,5},{5,4},{6,7},{7,6},{8,9},{9,8},{10,11... | collective-permute-start | bytes 6291464 | tf_op jit(solution)/shard_map/ppermute | solution.py:191
  210.1 53.8 %collective-permute-start.13 = (bf16[512,2048]{1,0:T(8,128)(2,1)}, bf16[512,2048]{1,0:T(8,128)(2,1)}, u32[]{:S(2)}, u32[]{:S(2)}) collective-permute-start(bf16[512,2048]{1,0:T(8,128)(2,1)} %collective-permute-done.12), channel_id=1, source_target_pairs={{0,1},{1,0},{2,3},{3,2},{4,5},{5,4},{6,7},{7,6},{8,9},{9,8},{10,11... | collective-permute-start | bytes 6291464 | tf_op jit(solution)/shard_map/ppermute | solution.py:191
  210.3 25.5 %collective-permute-start.8 = (bf16[2,1024,256]{2,1,0:T(8,128)(2,1)S(1)}, bf16[2,1024,256]{2,1,0:T(8,128)(2,1)S(1)}, u32[]{:S(2)}, u32[]{:S(2)}) collective-permute-start(bf16[2,1024,256]{2,1,0:T(8,128)(2,1)S(1)} %pad_maximum_fusion.5), channel_id=1, source_target_pairs={{0,16},{16,0},{1,17},{17,1},{2,18},{18,2},{3,19},{19,3},{4,20},{20... | collective-permute-start | bytes 3145736 | tf_op jit(solution)/shard_map/ppermute | solution.py:216
  237.5 48.6 %collective-permute-start.17 = (bf16[2,1024,512]{2,1,0:T(8,128)(2,1)}, bf16[2,1024,512]{2,1,0:T(8,128)(2,1)}, u32[]{:S(2)}, u32[]{:S(2)}) collective-permute-start(bf16[2,1024,512]{2,1,0:T(8,128)(2,1)} %pad_maximum_fusion.refs_0_), channel_id=1, source_target_pairs={{0,2},{1,3},{2,0},{3,1},{4,6},{5,7},{6,4},{7,5},{8,10},{9,11},{10,... | collective-permute-start | bytes 6291464 | tf_op jit(solution)/shard_map/ppermute | solution.py:191
  263.5 193.3 %reduce-scatter.4.cloned.1.call-start = ((), (), s32[]{:S(2)}) async-start(), calls=%async_computation.6 | async-start | bytes 7864320 | tf_op jit(solution)/shard_map/reduce_scatter | solution.py:322
  263.8 37.3 %collective-permute-start.16 = (bf16[2,1024,512]{2,1,0:T(8,128)(2,1)}, bf16[2,1024,512]{2,1,0:T(8,128)(2,1)}, u32[]{:S(2)}, u32[]{:S(2)}) collective-permute-start(bf16[2,1024,512]{2,1,0:T(8,128)(2,1)} %pad_maximum_fusion.refs_0_), channel_id=1, source_target_pairs={{0,1},{1,0},{2,3},{3,2},{4,5},{5,4},{6,7},{7,6},{8,9},{9,8},{10,11... | collective-permute-start | bytes 6291464 | tf_op jit(solution)/shard_map/ppermute | solution.py:191
  263.9 8.1 copy-start.6
  286.2 15.0 %collective-permute-start.18 = (bf16[2,1024,512]{2,1,0:T(8,128)(2,1)}, bf16[2,1024,512]{2,1,0:T(8,128)(2,1)S(1)}, u32[]{:S(2)}, u32[]{:S(2)}) collective-permute-start(bf16[2,1024,512]{2,1,0:T(8,128)(2,1)} %collective-permute-done.17.refs_2_), channel_id=1, source_target_pairs={{0,1},{1,0},{2,3},{3,2},{4,5},{5,4},{6,7},{7,6},{8,9},{9,8},{10,11... | collective-permute-start | bytes 6291464 | tf_op jit(solution)/shard_map/ppermute | solution.py:191
  287.4 13.7 %copy-start.4 = (bf16[768,2048]{1,0:T(8,128)(2,1)}, bf16[768,2048]{1,0:T(8,128)(2,1)S(1)}, u32[]{:S(2)}) copy-start(bf16[768,2048]{1,0:T(8,128)(2,1)S(1)} %fusion.13) | copy-start | bytes 9437188
  325.2 245.1 %reduce-scatter.6.cloned.1.call-start = ((), (), s32[]{:S(2)}) async-start(), calls=%async_computation.8 | async-start | bytes 7864320 | tf_op jit(solution)/shard_map/reduce_scatter | solution.py:342
  367.8 7.5 collective-permute-start.19
  372.8 9.4 %collective-permute-start.20 = (f32[512,2048]{1,0:T(8,128)}, f32[512,2048]{1,0:T(8,128)}, u32[]{:S(2)}, u32[]{:S(2)}) collective-permute-start(f32[512,2048]{1,0:T(8,128)} %fusion.67), channel_id=1, source_target_pairs={{0,1},{1,0},{2,3},{3,2},{4,5},{5,4},{6,7},{7,6},{8,9},{9,8},{10,11... | collective-permute-start | bytes 12582920 | tf_op jit(solution)/shard_map/ppermute | solution.py:191
  456.9 356.0 %reduce-scatter.8.cloned.1.call-start = ((), (), s32[]{:S(2)}) async-start(), calls=%async_computation.9 | async-start | bytes 7864320 | tf_op jit(solution)/shard_map/reduce_scatter | solution.py:361
  462.8 7.5 collective-permute-start.21
  462.8 93.3 %collective-permute-start.22 = (f32[1024,1024]{1,0:T(8,128)}, f32[1024,1024]{1,0:T(8,128)}, u32[]{:S(2)}, u32[]{:S(2)}) collective-permute-start(f32[1024,1024]{1,0:T(8,128)} %convolution_add_fusion.3), channel_id=1, source_target_pairs={{0,2},{1,3},{2,0},{3,1},{4,6},{5,7},{6,4},{7,5},{8,10},{9,11},{10,... | collective-permute-start | bytes 12582920 | tf_op jit(solution)/shard_map/ppermute | solution.py:191
  574.9 6.6 copy-start.10
  583.3 9.9 %collective-permute-start.23 = (bf16[192,512]{1,0:T(8,128)(2,1)}, bf16[192,512]{1,0:T(8,128)(2,1)S(1)}, u32[]{:S(2)}, u32[]{:S(2)}) collective-permute-start(bf16[192,512]{1,0:T(8,128)(2,1)} %get-tuple-element.110), channel_id=1, source_target_pairs={{0,4},{4,8},{8,12},{12,0},{1,5},{5,9},{9,13},{13,1},{2,6},{6,10},{... | collective-permute-start | bytes 589832 | tf_op jit(solution)/shard_map/ppermute | solution.py:194
  584.8 15.7 %collective-permute-start.24 = (bf16[192,512]{1,0:T(8,128)(2,1)}, bf16[192,512]{1,0:T(8,128)(2,1)S(1)}, u32[]{:S(2)}, u32[]{:S(2)}) collective-permute-start(bf16[192,512]{1,0:T(8,128)(2,1)} %get-tuple-element.109), channel_id=1, source_target_pairs={{0,8},{4,12},{8,0},{12,4},{1,9},{5,13},{9,1},{13,5},{2,10},{6,14},... | collective-permute-start | bytes 589832 | tf_op jit(solution)/shard_map/ppermute | solution.py:194
  586.5 14.6 %collective-permute-start.25 = (bf16[192,512]{1,0:T(8,128)(2,1)}, bf16[192,512]{1,0:T(8,128)(2,1)S(1)}, u32[]{:S(2)}, u32[]{:S(2)}) collective-permute-start(bf16[192,512]{1,0:T(8,128)(2,1)} %get-tuple-element.108), channel_id=1, source_target_pairs={{0,12},{4,0},{8,4},{12,8},{1,13},{5,1},{9,5},{13,9},{2,14},{6,2},{... | collective-permute-start | bytes 589832 | tf_op jit(solution)/shard_map/ppermute | solution.py:194
  631.6 12.0 %collective-permute-start.29 = (f32[512,2048]{1,0:T(8,128)}, f32[512,2048]{1,0:T(8,128)}, u32[]{:S(2)}, u32[]{:S(2)}) collective-permute-start(f32[512,2048]{1,0:T(8,128)} %fusion.63), channel_id=1, source_target_pairs={{0,1},{1,0},{2,3},{3,2},{4,5},{5,4},{6,7},{7,6},{8,9},{9,8},{10,11... | collective-permute-start | bytes 12582920 | tf_op jit(solution)/shard_map/ppermute | solution.py:191
  631.6 93.3 %collective-permute-start.30 = (f32[512,2048]{1,0:T(8,128)}, f32[512,2048]{1,0:T(8,128)}, u32[]{:S(2)}, u32[]{:S(2)}) collective-permute-start(f32[512,2048]{1,0:T(8,128)} %convolution_add_fusion.2), channel_id=1, source_target_pairs={{0,2},{1,3},{2,0},{3,1},{4,6},{5,7},{6,4},{7,5},{8,10},{9,11},{10,... | collective-permute-start | bytes 12582920 | tf_op jit(solution)/shard_map/ppermute | solution.py:191
  637.8 164.8 %collective-permute-start.40 = (f32[512,1536]{1,0:T(8,128)S(1)}, f32[512,1536]{1,0:T(8,128)S(1)}, u32[]{:S(2)}, u32[]{:S(2)}) collective-permute-start(f32[512,1536]{1,0:T(8,128)S(1)} %fusion.57), channel_id=1, source_target_pairs={{0,1},{1,0},{2,3},{3,2},{4,5},{5,4},{6,7},{7,6},{8,9},{9,8},{10,11... | collective-permute-start | bytes 9437192 | tf_op jit(solution)/shard_map/ppermute | solution.py:191
  643.7 87.3 %copy-start.16 = (bf16[1024,1024]{1,0:T(8,128)(2,1)S(1)}, bf16[1024,1024]{1,0:T(8,128)(2,1)}, u32[]{:S(2)}) copy-start(bf16[1024,1024]{1,0:T(8,128)(2,1)} %add_convert_fusion.2) | copy-start | bytes 6291460
  731.0 11.7 %copy-start.2 = (bf16[768,1536]{1,0:T(8,128)(2,1)S(1)}, bf16[768,1536]{1,0:T(8,128)(2,1)}, u32[]{:S(2)}) copy-start(bf16[768,1536]{1,0:T(8,128)(2,1)} %attn_bwd.1) | copy-start | bytes 7077892
  731.2 71.1 %collective-permute-start.46 = (bf16[1024,512]{1,0:T(8,128)(2,1)S(1)}, bf16[1024,512]{1,0:T(8,128)(2,1)S(1)}, u32[]{:S(2)}, u32[]{:S(2)}) collective-permute-start(bf16[1024,512]{1,0:T(8,128)(2,1)S(1)} %get-tuple-element.91), channel_id=1, source_target_pairs={{0,8},{4,9},{8,10},{12,11},{1,12},{5,13},{9,14},{13,15},{2,0},{6,1... | collective-permute-start | bytes 3145736 | tf_op jit(solution)/shard_map/ppermute | solution.py:203
  734.3 68.0 %collective-permute-start.45 = (bf16[1024,512]{1,0:T(8,128)(2,1)S(1)}, bf16[1024,512]{1,0:T(8,128)(2,1)S(1)}, u32[]{:S(2)}, u32[]{:S(2)}) collective-permute-start(bf16[1024,512]{1,0:T(8,128)(2,1)S(1)} %get-tuple-element.90), channel_id=1, source_target_pairs={{4,1},{8,2},{12,3},{1,4},{9,6},{13,7},{2,8},{6,9},{14,11},{3,12},{... | collective-permute-start | bytes 3145736 | tf_op jit(solution)/shard_map/ppermute | solution.py:203
  735.2 46.9 %collective-permute-start.26 = (bf16[192,512]{1,0:T(8,128)(2,1)S(1)}, bf16[192,512]{1,0:T(8,128)(2,1)S(1)}, u32[]{:S(2)}, u32[]{:S(2)}) collective-permute-start(bf16[192,512]{1,0:T(8,128)(2,1)S(1)} %get-tuple-element.106), channel_id=1, source_target_pairs={{0,4},{4,8},{8,12},{12,0},{1,5},{5,9},{9,13},{13,1},{2,6},{6,10},{... | collective-permute-start | bytes 589832 | tf_op jit(solution)/shard_map/ppermute | solution.py:194
  741.5 55.6 %collective-permute-start.27 = (bf16[192,512]{1,0:T(8,128)(2,1)S(1)}, bf16[192,512]{1,0:T(8,128)(2,1)S(1)}, u32[]{:S(2)}, u32[]{:S(2)}) collective-permute-start(bf16[192,512]{1,0:T(8,128)(2,1)S(1)} %get-tuple-element.105), channel_id=1, source_target_pairs={{0,8},{4,12},{8,0},{12,4},{1,9},{5,13},{9,1},{13,5},{2,10},{6,14},... | collective-permute-start | bytes 589832 | tf_op jit(solution)/shard_map/ppermute | solution.py:194
  782.1 20.2 %collective-permute-start.28 = (bf16[192,512]{1,0:T(8,128)(2,1)S(1)}, bf16[192,512]{1,0:T(8,128)(2,1)S(1)}, u32[]{:S(2)}, u32[]{:S(2)}) collective-permute-start(bf16[192,512]{1,0:T(8,128)(2,1)S(1)} %get-tuple-element.104), channel_id=1, source_target_pairs={{0,12},{4,0},{8,4},{12,8},{1,13},{5,1},{9,5},{13,9},{2,14},{6,2},{... | collective-permute-start | bytes 589832 | tf_op jit(solution)/shard_map/ppermute | solution.py:194
  797.1 104.6 %collective-permute-start.39 = (f32[512,1536]{1,0:T(8,128)}, f32[512,1536]{1,0:T(8,128)}, u32[]{:S(2)}, u32[]{:S(2)}) collective-permute-start(f32[512,1536]{1,0:T(8,128)} %fusion.60), channel_id=1, source_target_pairs={{0,1},{1,0},{2,3},{3,2},{4,5},{5,4},{6,7},{7,6},{8,9},{9,8},{10,11... | collective-permute-start | bytes 9437192 | tf_op jit(solution)/shard_map/ppermute | solution.py:191
  807.1 94.6 %collective-permute-start.41 = (f32[512,1536]{1,0:T(8,128)}, f32[512,1536]{1,0:T(8,128)}, u32[]{:S(2)}, u32[]{:S(2)}) collective-permute-start(f32[512,1536]{1,0:T(8,128)} %convolution_add_fusion), channel_id=1, source_target_pairs={{0,2},{1,3},{2,0},{3,1},{4,6},{5,7},{6,4},{7,5},{8,10},{9,11},{10,... | collective-permute-start | bytes 9437192 | tf_op jit(solution)/shard_map/ppermute | solution.py:191
  810.8 8.7 collective-permute-start.43
  813.0 11.2 %copy-start.13 = (bf16[768,2048]{1,0:T(8,128)(2,1)S(1)}, bf16[768,2048]{1,0:T(8,128)(2,1)}, u32[]{:S(2)}) copy-start(bf16[768,2048]{1,0:T(8,128)(2,1)} %all-gather.9.cloned.1.call-done) | copy-start | bytes 9437188
  815.4 5.3 collective-permute-start.36
  818.2 4.6 collective-permute-start.35
  819.4 8.7 collective-permute-start.33
  820.7 7.7 collective-permute-start.32
  822.7 12.8 %copy-start.26 = (f32[2048]{0:T(1024)S(1)}, f32[2048]{0:T(1024)}, u32[]{:S(2)}) copy-start(f32[2048]{0:T(1024)} %get-tuple-element.133) | copy-start | bytes 24580
  822.7 5.4 collective-permute-start.34
  828.1 7.5 collective-permute-start.42
  828.2 71.4 %collective-permute-start.44 = (f32[512,512]{1,0:T(8,128)S(1)}, f32[512,512]{1,0:T(8,128)S(1)}, u32[]{:S(2)}, u32[]{:S(2)}) collective-permute-start(f32[512,512]{1,0:T(8,128)S(1)} %convolution_add_fusion.4), channel_id=1, source_target_pairs={{0,2},{1,3},{2,0},{3,1},{4,6},{5,7},{6,4},{7,5},{8,10},{9,11},{10,... | collective-permute-start | bytes 3145736 | tf_op jit(solution)/shard_map/ppermute | solution.py:191
  828.4 5.4 collective-permute-start.31
  833.9 67.9 %copy-start.3 = (bf16[768,1536]{1,0:T(8,128)(2,1)S(1)}, bf16[768,1536]{1,0:T(8,128)(2,1)}, u32[]{:S(2)}) copy-start(bf16[768,1536]{1,0:T(8,128)(2,1)} %attn_bwd.1) | copy-start | bytes 7077892
  835.6 65.4 %collective-permute-start.37 = (f32[6656]{0:T(1024)S(1)}, f32[6656]{0:T(1024)S(1)}, u32[]{:S(2)}, u32[]{:S(2)}) collective-permute-start(f32[6656]{0:T(1024)S(1)} %pad_maximum_fusion.10), channel_id=1, source_target_pairs={{0,1},{1,0},{2,3},{3,2},{4,5},{5,4},{6,7},{7,6},{8,9},{9,8},{10,11... | collective-permute-start | bytes 79880 | tf_op jit(solution)/shard_map/ppermute | solution.py:191
  901.0 6.6 collective-permute-start.38
  901.7 7.8 copy-start.1
  (20 other events, 59.7 us)
Sparse Core Ops, SparseCore 0:
  10.1 30.6 all-gather.4
  42.5 64.1 all-gather.6
  134.0 103.5 all-gather.8
  263.7 70.3 all-gather.10
  336.2 120.6 reduce-scatter.3
  459.0 111.2 reduce-scatter.5
  626.8 114.5 reduce-scatter.7
